TPU v7x, 8 devices: a whole 2x2x1 slice. The times are simulated.
8 devices in a mesh: dp: 2 (over z, y), ep: 4 (over x, core).
Axes of the slice: x: 2, y: 2, z: 1, core: 2. Of those that a mesh axis runs over, the one named last changes fastest.
Arguments:
- tokens: bfloat16 [65536, 768], P(('dp', 'ep')), parts along dimension 0
- choice_idx: int32 [256, 256], P(('dp', 'ep')), parts along dimension 0
- gate_weight: float32 [256, 256], P(('dp', 'ep')), parts along dimension 0
- w_in: bfloat16 [128, 768, 3072], P('ep')
- w_out: bfloat16 [128, 3072, 768], P('ep')
Outputs:
- output: bfloat16 [65536, 768], P(('dp', 'ep')), parts along dimension 0
There are 2 independent parts. A program takes and returns all parts, laid end to end along the dimension named above; an argument that names none is the same for every part.
All inputs are finite; a program needn't handle non-finite values.
Results may differ from a plain program's by a relative error of at most 0.001.
Values are sent between devices in bfloat16 or wider.
A program may use at most 1.25 GiB of HBM per device.

v0:
```python
import jax
import jax.numpy as jnp
from jax import lax
from jax.sharding import PartitionSpec as P


def solution(mesh):
    group_n = mesh.shape["ep"]
    row_spec = P(("dp", "ep"), None)
    expert_spec = P("ep", None, None)

    def local_layer(tok_loc, sel_loc, gate_loc, win_loc, wout_loc):
        tok_count, model_dim = tok_loc.shape
        exp_count, cap_slots = sel_loc.shape
        slot_total = exp_count * cap_slots
        pair_cap = 2 * slot_total // group_n
        flat_sel = sel_loc.reshape(slot_total)
        src_dev = flat_sel // tok_count
        src_row = flat_sel % tok_count
        slot_order = jnp.argsort(src_dev, stable=True)
        counts = jax.ops.segment_sum(jnp.ones_like(src_dev), src_dev, num_segments=group_n)
        starts = jnp.cumsum(counts) - counts
        lane_idx = jnp.arange(pair_cap, dtype=jnp.int32)
        is_valid = lane_idx[None, :] < counts[:, None]
        slot_of = slot_order[jnp.minimum(starts[:, None] + lane_idx[None, :], slot_total - 1)]
        request = jnp.where(is_valid, src_row[slot_of], 0)
        sorted_rank = jnp.zeros(slot_total, jnp.int32).at[slot_order].set(jnp.arange(slot_total, dtype=jnp.int32))
        recv_place = src_dev * pair_cap + sorted_rank - starts[src_dev]
        asked_rows = lax.all_to_all(request, "ep", 0, 0, tiled=True)
        send_rows = tok_loc[asked_rows]
        got_rows = lax.all_to_all(send_rows, "ep", 0, 0, tiled=True)
        expert_in = got_rows.reshape(group_n * pair_cap, model_dim)[recv_place].reshape(exp_count, cap_slots, model_dim)
        pre_act = jnp.einsum("ecd,edf->ecf", expert_in, win_loc, preferred_element_type=jnp.float32)
        hidden = jax.nn.gelu(pre_act, approximate=True).astype(jnp.bfloat16)
        expert_out = jnp.einsum("ecf,efd->ecd", hidden, wout_loc, preferred_element_type=jnp.float32)
        weighted = (gate_loc[:, :, None] * expert_out).astype(jnp.bfloat16).reshape(slot_total, model_dim)
        back_rows = jnp.where(is_valid[:, :, None], weighted[slot_of], jnp.zeros((), jnp.bfloat16))
        returned = lax.all_to_all(back_rows, "ep", 0, 0, tiled=True)
        added = jax.ops.segment_sum(returned.reshape(group_n * pair_cap, model_dim).astype(jnp.float32), asked_rows.reshape(group_n * pair_cap), num_segments=tok_count)
        return (tok_loc.astype(jnp.float32) + added).astype(jnp.bfloat16)

    return jax.shard_map(local_layer, mesh=mesh, in_specs=(row_spec, row_spec, row_spec, expert_spec, expert_spec), out_specs=row_spec, check_vma=False)
```

profile of v0, /device:TPU:0, one launch (start us, length us, event | category | flops | bytes accessed | tf_op | source)
XLA Modules:
  0.0 1333.6 jit_solution(7665721385598280898)
XLA Ops:
  0.0 0.8 copy.6
  0.8 0.1 and_select_fusion
  1.0 57.0 %scatter_custom_fusion = s32[4]{0:T(128)S(1)} fusion(s32[8192]{0:T(1024)S(1)} %bitcast.56, s32[8192]{0:T(1024)S(1)} %broadcast.241, s32[]{:T(128)} %constant.18.clone.1), kind=kCustom, calls=%fused_computation.56 | custom fusion | flops 8192 | bytes 20 | tf_op jit(solution)/shard_map/scatter-add | solution.py:21
  58.0 0.2 reduce-window.9
  58.1 0.7 fusion.29
  58.8 0.2 compare_select_fusion.2
  59.0 0.8 copy.7
  59.8 6.8 sort.17
  66.6 90.5 %gather_fusion = s32[16384]{0:T(1024)S(1)} fusion(s32[8192]{0:T(1024)S(1)} %get-tuple-element.6, s32[16384]{0:T(1024)S(1)} %broadcast_clamp_fusion.1), kind=kCustom, calls=%fused_computation | custom fusion | bytes 196608 | tf_op jit(solution)/shard_map/gather | solution.py:25
  157.2 0.1 compare_select_fusion.1
  157.3 0.0 copy-start
  157.3 30.5 %scatter_custom_fusion.1 = s32[8192]{0:T(1024)S(1)} fusion(s32[8192]{0:T(1024)S(1)} %compare_select_fusion.9, s32[8192]{0:T(1024)S(1)} %iota.21, s32[]{:T(128)} %constant.18.clone.1), kind=kCustom, calls=%fused_computation.53 | custom fusion | bytes 32772 | tf_op jit(solution)/shard_map/scatter | solution.py:27
  187.8 2.7 compare_select_fusion.5
  190.6 90.5 %gather_fusion.1 = s32[16384]{0:T(1024)S(1)} fusion(s32[8192]{0:T(1024)S(1)} %get-tuple-element.8, s32[16384]{0:T(1024)S(1)} %broadcast_clamp_fusion.2), kind=kCustom, calls=%fused_computation.1 | custom fusion | bytes 196608 | tf_op jit(solution)/shard_map/gather | solution.py:26
  281.1 0.1 compare_select_fusion.3
  281.2 8.5 all_to_all.19
  289.8 0.6 copy-done.2
  290.4 0.1 compare_select_fusion
  290.5 79.2 %gather_fusion.2 = bf16[16384,768]{1,0:T(8,128)(2,1)} fusion(bf16[8192,768]{1,0:T(8,128)(2,1)} %param.5, s32[16384]{0:T(1024)S(1)} %broadcast_clamp_fusion), kind=kCustom, calls=%fused_computation.2 | custom fusion | bytes 50397184 | tf_op jit(solution)/shard_map/gather | solution.py:30
  369.7 8.6 all-to-all-start.1
  378.3 0.7 iota_compare_fusion
  379.0 271.7 %all-to-all-done.1 = bf16[4,4096,768]{2,1,0:T(8,128)(2,1)} async-done(((bf16[4,4096,768]{2,1,0:T(8,128)(2,1)}), bf16[4,4096,768]{2,1,0:T(8,128)(2,1)}, u32[]{:S(2)}, u32[]{:S(2)}) %all-to-all-start.1) | async-done | bytes 25165856 | tf_op jit(solution)/shard_map/all_to_all | solution.py:31
  650.7 48.4 %gather_fusion.3 = bf16[8192,768]{1,0:T(8,128)(2,1)} fusion(bf16[16384,768]{1,0:T(8,128)(2,1)} %bitcast.11, s32[8192]{0:T(1024)S(1)} %get-tuple-element.7), kind=kCustom, calls=%fused_computation.3 | custom fusion | bytes 25198592 | tf_op jit(solution)/shard_map/gather | solution.py:32
  699.2 106.6 %multiply_convert_fusion = bf16[32,256,768]{2,1,0:T(8,128)(2,1)} fusion(f32[32,256]{1,0:T(8,128)S(1)} %copy-done.4, bf16[32,3072,768]{2,1,0:T(8,128)(2,1)} %param.9, bf16[32,256,768]{2,1,0:T(8,128)(2,1)} %bitcast.42, bf16[32,768,3072]{2,1,0:T(8,128)(2,1)} %param.8), kind=kOutput, calls=%fused_computation.24 | convolution fusion | flops 77548486656 | bytes 327188480 | tf_op jit(solution)/shard_map/ecf,efd->ecd/dot_general | solution.py:35
  805.8 0.0 copy-done.1
  805.8 79.3 %gather_fusion.4 = bf16[16384,768]{1,0:T(8,128)(2,1)} fusion(bf16[8192,768]{1,0:T(8,128)(2,1)} %bitcast.39, s32[16384]{0:T(1024)S(1)} %copy-done.1), kind=kCustom, calls=%fused_computation.4 | custom fusion | bytes 50397184 | tf_op jit(solution)/shard_map/gather | solution.py:37
  885.1 22.4 %broadcast_select_fusion = bf16[4,4096,768]{2,1,0:T(8,128)(2,1)} fusion(bf16[4,4096,768]{2,1,0:T(8,128)(2,1)} %bitcast.41, pred[4,4096]{1,0:T(4,128)(4,1)S(1)} %copy-done.3), kind=kLoop, calls=%fused_computation.25 | loop fusion | flops 12582912 | bytes 50348032 | tf_op jit(solution)/shard_map/jit(_where)/select_n | solution.py:37
  907.4 8.6 all-to-all-start.2
  916.1 14.3 %convert_element_type.18 = f32[8192,768]{1,0:T(8,128)} convert(bf16[8192,768]{1,0:T(8,128)(2,1)} %param.5) | non-fusion elementwise | flops 6291456 | bytes 37748736 | tf_op jit(solution)/shard_map/convert_element_type | solution.py:40
  930.4 258.3 %all-to-all-done.2 = bf16[4,4096,768]{2,1,0:T(8,128)(2,1)} async-done(((bf16[4,4096,768]{2,1,0:T(8,128)(2,1)}), bf16[4,4096,768]{2,1,0:T(8,128)(2,1)}, u32[]{:S(2)}, u32[]{:S(2)}) %all-to-all-start.2) | async-done | bytes 25165856 | tf_op jit(solution)/shard_map/all_to_all | solution.py:38
  1188.7 131.9 %scatter_custom_fusion.2 = f32[8192,768]{1,0:T(8,128)} fusion(f32[8192,768]{1,0:T(8,128)} %convert_element_type.18, s32[16384]{0:T(1024)} %bitcast.47, bf16[16384,768]{1,0:T(8,128)(2,1)} %bitcast.21), kind=kCustom, calls=%fused_computation.18 | custom fusion | flops 25165824 | bytes 50331648 | tf_op jit(solution)/shard_map/scatter-add | solution.py:39
  1320.5 13.1 convert_element_type.23
  (17 shorter events, 0.1 us)
Async XLA Ops:
  157.3 123.9 %copy-start = (s32[16384]{0:T(1024)}, s32[16384]{0:T(1024)S(1)}, u32[]{:S(2)}) copy-start(s32[16384]{0:T(1024)S(1)} %broadcast_clamp_fusion.2) | copy-start | bytes 196612
  289.8 0.6 copy-start.2
  369.7 281.0 %all-to-all-start.1 = ((bf16[4,4096,768]{2,1,0:T(8,128)(2,1)}), bf16[4,4096,768]{2,1,0:T(8,128)(2,1)}, u32[]{:S(2)}, u32[]{:S(2)}) async-start(bf16[4,4096,768]{2,1,0:T(8,128)(2,1)} %bitcast.40), calls=%async_computation.1 | async-start | bytes 50331648 | tf_op jit(solution)/shard_map/all_to_all | solution.py:31
  650.7 48.4 %copy-start.4 = (f32[32,256]{1,0:T(8,128)S(1)}, f32[32,256]{1,0:T(8,128)}, u32[]{:S(2)}) copy-start(f32[32,256]{1,0:T(8,128)} %param.7) | copy-start | bytes 98308
  699.2 106.6 %copy-start.1 = (s32[16384]{0:T(1024)S(1)}, s32[16384]{0:T(1024)}, u32[]{:S(2)}) copy-start(s32[16384]{0:T(1024)} %copy-done) | copy-start | bytes 196612
  805.8 79.3 %copy-start.3 = (pred[4,4096]{1,0:T(4,128)(4,1)S(1)}, pred[4,4096]{1,0:T(4,128)(4,1)}, u32[]{:S(2)}) copy-start(pred[4,4096]{1,0:T(4,128)(4,1)} %iota_compare_fusion) | copy-start | bytes 49156
  907.4 281.2 %all-to-all-start.2 = ((bf16[4,4096,768]{2,1,0:T(8,128)(2,1)}), bf16[4,4096,768]{2,1,0:T(8,128)(2,1)}, u32[]{:S(2)}, u32[]{:S(2)}) async-start(bf16[4,4096,768]{2,1,0:T(8,128)(2,1)} %broadcast_select_fusion), calls=%async_computation.2 | async-start | bytes 50331648 | tf_op jit(solution)/shard_map/all_to_all | solution.py:38
where the time goes:
time: 1330 us
  waiting for transfers between devices  530 us (40%)
  local copies, waits for them, and re-layouts  421 us (32%)
  other arithmetic  250 us (19%)
  matrix products  107 us (8%)
  starting transfers between devices  17.2 us (1%)
    all_to_all x1, waiting for transfers between devices, local_layer(): got_rows = lax.all_to_all(send_rows, 'ep', 0, 0, tiled=True)  272 us
    all_to_all x1, waiting for transfers between devices, local_layer(): returned = lax.all_to_all(back_rows, 'ep', 0, 0, tiled=True)  258 us
    scatter-add x1, other arithmetic, local_layer(): jax.ops.segment_sum(returned.reshape(group_n * pair_cap, model_dim).astyp...  132 us
    dot_general x1, matrix products, local_layer(): jnp.einsum('ecf,efd->ecd', hidden, wout_loc, preferred_element_type=jnp.f...  107 us
    gather x1, local copies, waits for them, and re-layouts, local_layer(): slot_order[jnp.minimum(starts[:, None] + lane_idx[None, :], slot_total - 1)]  90.5 us
    gather x1, local copies, waits for them, and re-layouts, local_layer(): request = jnp.where(is_valid, src_row[slot_of], 0)  90.5 us
    gather x1, local copies, waits for them, and re-layouts, local_layer(): weighted[slot_of]  79.3 us
    gather x1, local copies, waits for them, and re-layouts, local_layer(): send_rows = tok_loc[asked_rows]  79.2 us
  transfers between devices with their start and end apart: 2, of which 2 were waited for; matrix products, arithmetic and copies ran while one was open for 1% of the time, Pallas kernels for 0%

commit v1 on v0

v1 whole, which is shorter than its diff:
```python
import functools

import jax
import jax.numpy as jnp
from jax import lax
from jax.experimental import pallas as pl
from jax.experimental.pallas import tpu as pltpu
from jax.sharding import PartitionSpec as P

LANES = 128
ROW = 8
BLOCK = 512
STEP = 512


def one_hot(index, size):
    return index[..., None] == jnp.arange(size, dtype=index.dtype)


def bdot(spec, a, b):
    return jnp.einsum(spec, a.astype(jnp.bfloat16), b.astype(jnp.bfloat16), preferred_element_type=jnp.float32)


def exclusive_rank(flags):
    rows, cols = flags.shape
    f = flags.astype(jnp.float32)
    before = jnp.arange(cols)[:, None] < jnp.arange(cols)[None, :]
    inside = bdot("hl,lm->hm", f, before)
    row_sum = f.sum(1)
    above = jnp.arange(rows)[:, None] < jnp.arange(rows)[None, :]
    offset = bdot("h,hm->m", row_sum, above)
    return (inside + offset[:, None]).astype(jnp.int32), row_sum.sum().astype(jnp.int32)


def invert(flags, rank, value, size):
    high = (one_hot(rank // LANES, size // LANES) & flags[:, None]).astype(jnp.bfloat16)
    low = one_hot(rank % LANES, LANES)
    vh = jnp.where(low, (value // LANES)[:, None], 0)
    vl = jnp.where(low, (value % LANES)[:, None], 0)
    th = bdot("kh,kl->hl", high, vh)
    tl = bdot("kh,kl->hl", high, vl)
    return (th * LANES + tl).astype(jnp.int32).reshape(size)


def lookup(table, index):
    high = one_hot(index // LANES, table.shape[0]).astype(jnp.bfloat16)
    low = one_hot(index % LANES, LANES)
    th = bdot("kh,hl->kl", high, table // LANES)
    tl = bdot("kh,hl->kl", high, table % LANES)
    return jnp.where(low, th * LANES + tl, 0).sum(1).astype(jnp.int32)


def combine_kernel(first, dest_ref, dup_ref, tok_ref, own_ref, sib_ref, ra_ref, rb_ref, out_ref, acc, rows):
    i = pl.program_id(0)
    lane_blocks = tok_ref.shape[1] // LANES
    t0, t1, t2, t3, t4, t5 = first

    @pl.when(i < t1)
    def _():
        base = i * BLOCK * ROW
        for k in range(lane_blocks):
            acc[pl.ds(base + k, BLOCK, stride=ROW), :] = tok_ref[:, k * LANES:(k + 1) * LANES].astype(jnp.float32)

    def add(src, step):
        for k in range(lane_blocks):
            rows[pl.ds(k, BLOCK, stride=ROW), :] = src[:, k * LANES:(k + 1) * LANES].astype(jnp.float32)
        start = step * BLOCK

        def spot(r):
            return pl.ds(pl.multiple_of(dest_ref[start + r] * ROW, ROW), ROW)

        def line(r):
            return pl.ds(pl.multiple_of(r * ROW, ROW), ROW)

        @pl.when(dup_ref[step] == 0)
        def _():
            def body(j, c):
                where = [spot(j * 8 + u) for u in range(8)]
                sums = [acc[where[u], :] + rows[line(j * 8 + u), :] for u in range(8)]
                for u in range(8):
                    acc[where[u], :] = sums[u]
                return c
            lax.fori_loop(0, BLOCK // 8, body, 0)

        @pl.when(dup_ref[step] != 0)
        def _():
            def body(r, c):
                w = spot(r)
                acc[w, :] = acc[w, :] + rows[line(r), :]
                return c
            lax.fori_loop(0, BLOCK, body, 0)

    for lo, hi, ref in ((t1, t2, own_ref), (t2, t3, sib_ref), (t3, t4, ra_ref), (t4, t5, rb_ref)):
        @pl.when((i >= lo) & (i < hi))
        def _(ref=ref):
            add(ref, i - t1)

    @pl.when(i >= t5)
    def _():
        base = (i - t5) * BLOCK * ROW
        for k in range(lane_blocks):
            out_ref[:, k * LANES:(k + 1) * LANES] = acc[pl.ds(base + k, BLOCK, stride=ROW), :].astype(out_ref.dtype)


def combine(tok, parts, dest):
    n, d = tok.shape
    counts = [n // BLOCK] + [p.shape[0] // BLOCK for p in parts] + [n // BLOCK]
    first = [0]
    for c in counts:
        first.append(first[-1] + c)
    groups = dest.reshape(-1, 8)
    same = (groups[:, :, None] == groups[:, None, :]) & (groups[:, :, None] < n) & (jnp.arange(8)[:, None] < jnp.arange(8)[None, :])
    dup = same.reshape(-1, BLOCK * 8).any(1).astype(jnp.int32)

    def spec(k):
        return pl.BlockSpec((BLOCK, d), lambda i, *_: (jnp.clip(i - first[k], 0, counts[k] - 1), 0))

    return pl.pallas_call(
        functools.partial(combine_kernel, first[:6]),
        grid_spec=pltpu.PrefetchScalarGridSpec(
            num_scalar_prefetch=2,
            grid=(first[-1],),
            in_specs=[spec(k) for k in range(5)],
            out_specs=spec(5),
            scratch_shapes=[pltpu.VMEM(((n + 1) * ROW, LANES), jnp.float32), pltpu.VMEM((BLOCK * ROW, LANES), jnp.float32)],
        ),
        out_shape=jax.ShapeDtypeStruct((n, d), tok.dtype),
        compiler_params=pltpu.CompilerParams(dimension_semantics=("arbitrary",), vmem_limit_bytes=60 * 2**20),
        name="combine",
    )(dest, dup, tok, *parts)


def solution(mesh):
    group_n = mesh.shape["ep"]
    row_spec = P(("dp", "ep"), None)
    expert_spec = P("ep", None, None)
    swap_core = [(g, g ^ 1) for g in range(group_n)]
    swap_chip = [(g, g ^ 2) for g in range(group_n)]

    def local_layer(tok_loc, sel_loc, gate_loc, win_loc, wout_loc):
        n, d = tok_loc.shape
        exp_count, cap_slots = sel_loc.shape
        slots = exp_count * cap_slots
        me = lax.axis_index("ep")
        chip, core = me // 2, me % 2
        chip_n = 2 * n
        half = chip_n // 2
        levels = list(range(STEP * 5, half + 1, STEP))

        sib_tok = lax.ppermute(tok_loc, "ep", swap_core)
        all_sel = lax.all_gather(sel_loc.reshape(slots), "ep").reshape(2, 2 * slots)
        chip_sel = lax.dynamic_index_in_dim(all_sel, chip, 0, keepdims=False)
        far_sel = lax.dynamic_index_in_dim(all_sel, 1 - chip, 0, keepdims=False)
        my_sel = sel_loc.reshape(slots)
        sib_sel = lax.dynamic_slice_in_dim(chip_sel, (1 - core) * slots, slots)

        def needed(sel, owner):
            idx = sel - owner * chip_n
            high = one_hot(idx // LANES, chip_n // LANES)
            count = bdot("kh,kl->hl", high, one_hot(idx % LANES, LANES))
            return count > 0

        give = needed(far_sel, chip)
        want = needed(chip_sel, 1 - chip)
        give_rank, give_n = exclusive_rank(give)
        want_rank, want_n = exclusive_rank(want)
        ids = jnp.arange(chip_n, dtype=jnp.int32)
        give_list = invert(give.reshape(-1), give_rank.reshape(-1), ids, chip_n)
        give_list = (give_list + core * n) % chip_n
        give_mine = lax.dynamic_index_in_dim(give_list.reshape(half, 2), core, 1, keepdims=False)
        rank_of_slot = lookup(want_rank, my_sel - (1 - chip) * chip_n)
        tok_dev = my_sel // n
        far_slot = tok_dev // 2 != chip

        chip_far = chip_sel // chip_n != chip
        far_back = far_sel // chip_n == chip
        back_rank, back_n = exclusive_rank(chip_far.reshape(-1, LANES))
        come_rank, come_n = exclusive_rank(far_back.reshape(-1, LANES))
        slot_ids = jnp.arange(2 * slots, dtype=jnp.int32)
        back_list = invert(chip_far, back_rank.reshape(-1), (slot_ids + core * slots) % (2 * slots), 2 * slots)
        back_mine = lax.dynamic_index_in_dim(back_list.reshape(-1, 2), core, 1, keepdims=False)
        come_tok = invert(far_back, come_rank.reshape(-1), jnp.clip(far_sel - chip * chip_n, 0, chip_n - 1), 2 * slots)
        come_tok = jnp.where(slot_ids < come_n, come_tok - core * n, n).reshape(-1, 2)
        come_a = lax.dynamic_index_in_dim(come_tok, core, 1, keepdims=False)
        come_b = lax.dynamic_index_in_dim(come_tok, 1 - core, 1, keepdims=False)

        most = lax.pmax(jnp.stack([jnp.maximum(give_n, want_n), jnp.maximum(back_n, come_n)]), ("dp", "ep"))
        level = jnp.clip((most + 2 * STEP - 1) // (2 * STEP) - levels[0] // STEP, 0, len(levels) - 1)

        def dispatch(rows):
            def run(tok, sib, lst, rank, sel, far):
                table = jnp.concatenate([tok, sib])
                sent = table[lst[:rows]]
                got = lax.ppermute(sent, "ep", swap_chip)
                sib_got = lax.ppermute(got, "ep", swap_core)
                whole = jnp.concatenate([tok, sib, got, sib_got])
                near_at = sel % n + jnp.where(sel // n == me, 0, n)
                far_at = 2 * n + rank // 2 + jnp.where(rank % 2 == core, 0, rows)
                return whole[jnp.where(far, far_at, near_at)]
            return run

        expert_in = lax.switch(level[0], [dispatch(r) for r in levels], tok_loc, sib_tok, give_mine, rank_of_slot, my_sel, far_slot)
        expert_in = expert_in.reshape(exp_count, cap_slots, d)
        pre_act = jnp.einsum("ecd,edf->ecf", expert_in, win_loc, preferred_element_type=jnp.float32)
        hidden = jax.nn.gelu(pre_act, approximate=True).astype(jnp.bfloat16)
        expert_out = jnp.einsum("ecf,efd->ecd", hidden, wout_loc, preferred_element_type=jnp.float32)
        weighted = (gate_loc[:, :, None] * expert_out).astype(jnp.bfloat16).reshape(slots, d)
        sib_weighted = lax.ppermute(weighted, "ep", swap_core)

        def place(v):
            return jnp.where((v >= 0) & (v < n), v, n)

        def back(rows):
            def run(tok, w, sw, lst, a, b, mine, sib):
                sent = jnp.concatenate([w, sw])[lst[:rows]]
                got = lax.ppermute(sent, "ep", swap_chip)
                sib_got = lax.ppermute(got, "ep", swap_core)
                dest = jnp.concatenate([mine, sib, a[:rows], b[:rows]])
                return combine(tok, [w, sw, got, sib_got], dest)
            return run

        return lax.switch(level[1], [back(r) for r in levels], tok_loc, weighted, sib_weighted, back_mine,
                          place(come_a), place(come_b), place(my_sel - me * n), place(sib_sel - me * n))

    return jax.shard_map(local_layer, mesh=mesh, in_specs=(row_spec, row_spec, row_spec, expert_spec, expert_spec), out_specs=row_spec, check_vma=False)
```

time: 1330 us -> 1270 us (0.955); the launches traced: 1330 us -> 1250 us
  local copies, waits for them, and re-layouts: 421 us -> 246 us
  Pallas kernels: 0 us -> 121 us
  waiting for transfers between devices: 530 us -> 414 us
  other arithmetic: 250 us -> 165 us
  matrix products: 107 us -> 191 us
  loops' own time: 0 us -> 55.6 us
  blocking collectives: 8.53 us -> 45.2 us
    all_to_all x2 -> x0, waiting for transfers between devices: 530 us -> none  [the longest x1 272 us: local_layer(): got_rows = lax.all_to_all(send_rows, 'ep', 0, 0, tiled=True)]
    ppermute x0 -> x6, waiting for transfers between devices: none -> 414 us  [the longest x2 389 us: run(): got = lax.ppermute(sent, 'ep', swap_chip)]
    scatter-add x2 -> x0, other arithmetic: 189 us -> none  [the longest x1 132 us: local_layer(): jax.ops.segment_sum(returned.reshape(group_n * pair_cap, model_dim).astyp...]
    gather x6 -> x3, local copies, waits for them, and re-layouts: 389 us -> 213 us  [the longest x1 141 us: run(): return whole[jnp.where(far, far_at, near_at)]]
    concatenate x0 -> x4, other arithmetic: none -> 142 us  [the longest x1 91 us: run(): whole = jnp.concatenate([tok, sib, got, sib_got])]
    pallas_call x0 -> x1, Pallas kernels: none -> 121 us  [combine(): pl.pallas_call(functools.partial(combine_kernel, first[:6]), grid_spec=pl...]
    dot_general x0 -> x18, matrix products: none -> 83.8 us  [bdot(): jnp.einsum(spec, a.astype(jnp.bfloat16), b.astype(jnp.bfloat16), preferre...]
    another operation x0 -> x2, loops' own time: none -> 55.6 us  [the longest x1 29 us: local_layer(): lax.switch(level[1], [back(r) for r in levels], tok_loc, weighted, sib_we...]
  transfers between devices with their start and end apart: 2 -> 6, of which waited for: 2 -> 4; matrix products, arithmetic and copies ran while one was open for 1% -> 11% of each run, Pallas kernels for 0% -> 0%
where the time goes in v1:
time: 1270 us; the launch traced here: 1250 us
  waiting for transfers between devices  414 us (33%)
  local copies, waits for them, and re-layouts  246 us (19%)
  matrix products  191 us (15%)
  other arithmetic  165 us (13%)
  Pallas kernels  121 us (10%)
  loops' own time  55.6 us (4%)
  blocking collectives  45.2 us (4%)
    ppermute x2, waiting for transfers between devices, run(): got = lax.ppermute(sent, 'ep', swap_chip)  389 us
    gather x1, local copies, waits for them, and re-layouts, run(): return whole[jnp.where(far, far_at, near_at)]  141 us
    pallas_call x1, Pallas kernels, combine(): pl.pallas_call(functools.partial(combine_kernel, first[:6]), grid_spec=pl...  121 us
    dot_general x1, matrix products, local_layer(): jnp.einsum('ecf,efd->ecd', hidden, wout_loc, preferred_element_type=jnp.f...  107 us
    concatenate x1, other arithmetic, run(): whole = jnp.concatenate([tok, sib, got, sib_got])  91 us
    dot_general x18, matrix products, bdot(): jnp.einsum(spec, a.astype(jnp.bfloat16), b.astype(jnp.bfloat16), preferre...  83.8 us
    gather x1, local copies, waits for them, and re-layouts, run(): sent = jnp.concatenate([w, sw])[lst[:rows]]  39.4 us
    gather x1, local copies, waits for them, and re-layouts, run(): sent = table[lst[:rows]]  32.5 us
  transfers between devices with their start and end apart: 6, of which 4 were waited for; matrix products, arithmetic and copies ran while one was open for 11% of the time, Pallas kernels for 0%

profile of v1, /device:TPU:0, one launch (start us, length us, event | category | flops | bytes accessed | tf_op | source)
XLA Modules:
  0.0 1247.3 jit_solution(6774581451252093041)
XLA Ops:
  1.7 22.8 %all-gather = s32[4,1,8192]{2,1,0:T(1,128)S(1)} all-gather(s32[1,1,8192]{2,1,0:T(1,128)S(1)} %reshape.1218), channel_id=1, replica_groups=mesh['dp'=2,'ep'=4] {'ep'}, dimensions={0}, use_global_device_ids=true | all-gather | bytes 163840 | tf_op jit(solution)/shard_map/all_gather | solution.py:151
  31.4 5.3 convert_reduce_fusion
  40.2 5.4 fusion.346
  46.3 22.4 %pmax.7 = s32[2]{0:T(128)S(1)} all-reduce(s32[2]{0:T(128)S(1)} %pad_add_fusion.12), channel_id=1, replica_groups=mesh['dp'=2,'ep'=4] {'dp','ep'}, use_global_device_ids=true, to_apply=%region_4.5 | all-reduce | flops 2 | bytes 16 | tf_op jit(solution)/shard_map/pmax | solution.py:187
  69.3 11.2 fusion.167
  80.5 11.6 fusion.242
  92.1 5.5 add.635
  108.8 3.3 fusion.178
  112.2 521.5 %conditional.2 = (bf16[32,256,768]{2,1,0:T(8,128)(2,1)}) conditional(s32[]{:T(128)} %bitcast.24, (bf16[8192,768]{1,0:T(8,128)(2,1)}, bf16[8192,768]{1,0:T(8,128)(2,1)}, s32[8192]{0:T(1024)S(1)}, s32[8192]{0:T(1024)S(1)}, s32[]{:T(128)}, /*index=5*/s32[8192]{0:T(1024)S(1)}, s32[]{:T(128)}, ...), branch_computations={%region_8.9_spmd, %region_9.10_spmd, %region_10.11_spmd, %region_1... | conditional | flops 252100608 | bytes 352559200 | solution.py:202
  120.4 25.6 %pad_maximum_fusion.13 = bf16[16384,768]{1,0:T(8,128)(2,1)} fusion(bf16[8192,768]{1,0:T(8,128)(2,1)} %get-tuple-element.465, bf16[8192,768]{1,0:T(8,128)(2,1)} %get-tuple-element.464), kind=kLoop, calls=%fused_computation.205 | loop fusion | flops 50331648 | bytes 50331648 | tf_op jit(solution)/shard_map/cond/branch_6_fun/concatenate | solution.py:192
  146.0 32.5 %gather_fusion.12 = bf16[5632,768]{1,0:T(8,128)(2,1)} fusion(bf16[16384,768]{1,0:T(8,128)(2,1)} %pad_maximum_fusion.13, s32[6144]{0:T(1024)S(1)} %pad_clamp_fusion.3), kind=kCustom, calls=%fused_computation.12 | custom fusion | bytes 17324032 | tf_op jit(solution)/shard_map/cond/branch_6_fun/gather | solution.py:193
  180.7 185.3 %collective-permute-done.12 = bf16[5632,768]{1,0:T(8,128)(2,1)S(1)} collective-permute-done((bf16[5632,768]{1,0:T(8,128)(2,1)}, bf16[5632,768]{1,0:T(8,128)(2,1)S(1)}, u32[]{:S(2)}, u32[]{:S(2)}) %collective-permute-start.12) | collective-permute-done | bytes 8650784 | tf_op jit(solution)/shard_map/cond/branch_6_fun/ppermute | solution.py:194
  366.0 3.5 copy-done.5
  369.6 13.4 %collective-permute-done.13 = bf16[5632,768]{1,0:T(8,128)(2,1)} collective-permute-done((bf16[5632,768]{1,0:T(8,128)(2,1)S(1)}, bf16[5632,768]{1,0:T(8,128)(2,1)}, u32[]{:S(2)}, u32[]{:S(2)}) %collective-permute-start.13) | collective-permute-done | bytes 8650784 | tf_op jit(solution)/shard_map/cond/branch_6_fun/ppermute | solution.py:195
  383.0 91.0 %pad_maximum_fusion.12 = bf16[27648,768]{1,0:T(8,128)(2,1)} fusion(bf16[5632,768]{1,0:T(8,128)(2,1)} %collective-permute-done.13, bf16[5632,768]{1,0:T(8,128)(2,1)} %copy-done.5, bf16[8192,768]{1,0:T(8,128)(2,1)} %get-tuple-element.465, bf16[8192,768]{1,0:T(8,128)(2,1)} %get-tuple-element.464), kind=kLoop, calls=%fused_computation.204 | loop fusion | flops 169869312 | bytes 84934656 | tf_op jit(solution)/shard_map/cond/branch_6_fun/concatenate | solution.py:196
  474.0 141.3 %gather_fusion.13 = bf16[8192,768]{1,0:T(8,128)(2,1)} fusion(bf16[27648,768]{1,0:T(8,128)(2,1)} %pad_maximum_fusion.12, s32[8192]{0:T(1024)S(1)} %fusion.75), kind=kCustom, calls=%fused_computation.13 | custom fusion | bytes 25198592 | tf_op jit(solution)/shard_map/cond/branch_6_fun/gather | solution.py:199
  633.8 106.8 %multiply_convert_fusion = bf16[32,256,768]{2,1,0:T(8,128)(2,1)} fusion(f32[32,256]{1,0:T(8,128)S(1)} %copy-done.31, bf16[32,3072,768]{2,1,0:T(8,128)(2,1)} %param.33, bf16[32,256,768]{2,1,0:T(8,128)(2,1)} %get-tuple-element.665, bf16[32,768,3072]{2,1,0:T(8,128)(2,1)} %param.32), kind=kOutput, calls=%fused_computation.472 | convolution fusion | flops 77548486656 | bytes 327188480 | tf_op jit(solution)/shard_map/ecf,efd->ecd/dot_general | solution.py:206
  741.9 11.2 fusion.162
  753.1 11.6 fusion.254
  764.6 5.5 sub.280
  770.6 11.2 fusion.172
  781.8 11.3 fusion.230
  793.1 5.5 reshape_reshape.3
  798.6 4.4 dynamic-slice_reduce_fusion
  803.1 2.9 fusion.213
  805.9 4.4 dynamic-slice_reduce_fusion.1
  811.4 434.8 %conditional.3 = (bf16[8192,768]{1,0:T(8,128)(2,1)}) conditional(s32[]{:T(128)} %bitcast.18, (s32[8192]{0:T(1024)S(1)}, s32[8192]{0:T(1024)S(1)}, s32[8192]{0:T(1024)S(1)}, s32[8192]{0:T(1024)S(1)}, bf16[8192,768]{1,0:T(8,128)(2,1)}, /*index=5*/bf16[8192,768]{1,0:T(8,128)(2,1)}, s32[8192]{0:T(1024)S(1)}, ...), branch_computations={%region_22.25_spmd, %region_25.28_spmd, %region_28.31_spmd, %regio... | conditional | flops 51839040 | bytes 179094112 | solution.py:222
  825.4 25.6 %pad_maximum_fusion.31 = bf16[16384,768]{1,0:T(8,128)(2,1)} fusion(bf16[8192,768]{1,0:T(8,128)(2,1)} %get-tuple-element.574.sib_ref, bf16[8192,768]{1,0:T(8,128)(2,1)} %get-tuple-element.573.own_ref), kind=kLoop, calls=%fused_computation.421 | loop fusion | flops 50331648 | bytes 50331648 | tf_op jit(solution)/shard_map/cond/branch_7_fun/concatenate | solution.py:215
  851.0 39.4 %gather_fusion.31 = bf16[6144,768]{1,0:T(8,128)(2,1)} fusion(bf16[16384,768]{1,0:T(8,128)(2,1)} %pad_maximum_fusion.31, s32[6144]{0:T(1024)S(1)} %fusion.141), kind=kCustom, calls=%fused_computation.31 | custom fusion | bytes 18898944 | tf_op jit(solution)/shard_map/cond/branch_7_fun/gather | solution.py:215
  892.3 203.5 %collective-permute-done.38.ra_ref = bf16[6144,768]{1,0:T(8,128)(2,1)} collective-permute-done((bf16[6144,768]{1,0:T(8,128)(2,1)}, bf16[6144,768]{1,0:T(8,128)(2,1)}, u32[]{:S(2)}, u32[]{:S(2)}) %collective-permute-start.38) | collective-permute-done | bytes 9437216 | tf_op jit(solution)/shard_map/cond/branch_7_fun/ppermute | solution.py:216
  1099.1 11.3 collective-permute-done.39.rb_ref
  1110.4 120.9 %combine.19 = bf16[8192,768]{1,0:T(8,128)(2,1)} custom-call(s32[28672]{0:T(1024)} %copy-done.19, s32[56]{0:T(128)} %convert_element_type.129.dup_ref, bf16[8192,768]{1,0:T(8,128)(2,1)} %get-tuple-element.572.tok_ref, bf16[8192,768]{1,0:T(8,128)(2,1)} %get-tuple-element.573.own_ref, bf16[8192,768]{1,0:T(8,128)(2,1)} %get-tuple-element.574.sib_ref, ...), custom_call_target="tpu_custom_call" | custom-call | tf_op jit(solution)/shard_map/cond/branch_7_fun/combine/pallas_call | solution.py:118
  (84 shorter events, 30.8 us)
Async XLA Ops:
  0.0 68.8 %copy-start.28 = (s32[32,256]{1,0:T(8,128)S(1)}, s32[32,256]{1,0:T(8,128)}, u32[]{:S(2)}) copy-start(s32[32,256]{1,0:T(8,128)} %param.30) | copy-start | bytes 98308
  0.0 112.2 %collective-permute-start.48 = (bf16[8192,768]{1,0:T(8,128)(2,1)}, bf16[8192,768]{1,0:T(8,128)(2,1)}, u32[]{:S(2)}, u32[]{:S(2)}) collective-permute-start(bf16[8192,768]{1,0:T(8,128)(2,1)} %param.29), channel_id=1, source_target_pairs={{0,1},{1,0},{2,3},{3,2},{4,5},{5,4},{6,7},{7,6}} | collective-permute-start | bytes 37748744 | tf_op jit(solution)/shard_map/ppermute | solution.py:150
  24.9 2.4 copy-start.27
  26.5 0.8 copy-start.15
  26.5 54.0 %copy-start.17 = (s32[1,16384]{1,0:T(1,128)}, s32[1,16384]{1,0:T(1,128)S(1)}, u32[]{:S(2)}) copy-start(s32[1,16384]{1,0:T(1,128)S(1)} %get-tuple-element.624) | copy-start | bytes 196612
  112.2 521.5 %copy-start.31 = (f32[32,256]{1,0:T(8,128)S(1)}, f32[32,256]{1,0:T(8,128)}, u32[]{:S(2)}) copy-start(f32[32,256]{1,0:T(8,128)} %param.31) | copy-start | bytes 98308
  178.5 187.6 %collective-permute-start.12 = (bf16[5632,768]{1,0:T(8,128)(2,1)}, bf16[5632,768]{1,0:T(8,128)(2,1)S(1)}, u32[]{:S(2)}, u32[]{:S(2)}) collective-permute-start(bf16[5632,768]{1,0:T(8,128)(2,1)} %gather_fusion.12), channel_id=1, source_target_pairs={{0,2},{1,3},{2,0},{3,1},{4,6},{5,7},{6,4},{7,5}} | collective-permute-start | bytes 25952264 | tf_op jit(solution)/shard_map/cond/branch_6_fun/ppermute | solution.py:194
  366.0 3.5 copy-start.5
  369.5 13.5 %collective-permute-start.13 = (bf16[5632,768]{1,0:T(8,128)(2,1)S(1)}, bf16[5632,768]{1,0:T(8,128)(2,1)}, u32[]{:S(2)}, u32[]{:S(2)}) collective-permute-start(bf16[5632,768]{1,0:T(8,128)(2,1)S(1)} %collective-permute-done.12), channel_id=1, source_target_pairs={{0,1},{1,0},{2,3},{3,2},{4,5},{5,4},{6,7},{7,6}} | collective-permute-start | bytes 25952264 | tf_op jit(solution)/shard_map/cond/branch_6_fun/ppermute | solution.py:195
  633.7 107.5 %copy-start.16 = (s32[1,16384]{1,0:T(1,128)S(1)}, s32[1,16384]{1,0:T(1,128)}, u32[]{:S(2)}) copy-start(s32[1,16384]{1,0:T(1,128)} %copy-done.15) | copy-start | bytes 196612
  633.7 107.5 %copy-start.18 = (s32[1,16384]{1,0:T(1,128)S(1)}, s32[1,16384]{1,0:T(1,128)}, u32[]{:S(2)}) copy-start(s32[1,16384]{1,0:T(1,128)} %copy-done.17) | copy-start | bytes 196612
  633.7 108.1 %copy-start.30 = (s32[16384]{0:T(1024)S(1)}, s32[16384]{0:T(1024)}, u32[]{:S(2)}) copy-start(s32[16384]{0:T(1024)} %get-tuple-element.631) | copy-start | bytes 196612
  740.5 12.5 %copy-start.29 = (s32[16384]{0:T(1024)S(1)}, s32[16384]{0:T(1024)}, u32[]{:S(2)}) copy-start(s32[16384]{0:T(1024)} %get-tuple-element.629) | copy-start | bytes 196612
  740.5 70.9 %collective-permute-start.49 = (bf16[8192,768]{1,0:T(8,128)(2,1)}, bf16[8192,768]{1,0:T(8,128)(2,1)}, u32[]{:S(2)}, u32[]{:S(2)}) collective-permute-start(bf16[8192,768]{1,0:T(8,128)(2,1)} %bitcast.68), channel_id=1, source_target_pairs={{0,1},{1,0},{2,3},{3,2},{4,5},{5,4},{6,7},{7,6}} | collective-permute-start | bytes 37748744 | tf_op jit(solution)/shard_map/ppermute | solution.py:208
  793.1 18.3 %copy-start.6 = (s32[8192]{0:T(1024)S(1)}, s32[8192]{0:T(1024)}, u32[]{:S(2)}) copy-start(s32[8192]{0:T(1024)} %get-tuple-element.639) | copy-start | bytes 98308
  890.4 205.4 %collective-permute-start.38 = (bf16[6144,768]{1,0:T(8,128)(2,1)}, bf16[6144,768]{1,0:T(8,128)(2,1)}, u32[]{:S(2)}, u32[]{:S(2)}) collective-permute-start(bf16[6144,768]{1,0:T(8,128)(2,1)} %gather_fusion.31), channel_id=1, source_target_pairs={{0,2},{1,3},{2,0},{3,1},{4,6},{5,7},{6,4},{7,5}} | collective-permute-start | bytes 28311560 | tf_op jit(solution)/shard_map/cond/branch_7_fun/ppermute | solution.py:216
  1095.8 14.6 %collective-permute-start.39 = (bf16[6144,768]{1,0:T(8,128)(2,1)}, bf16[6144,768]{1,0:T(8,128)(2,1)}, u32[]{:S(2)}, u32[]{:S(2)}) collective-permute-start(bf16[6144,768]{1,0:T(8,128)(2,1)} %collective-permute-done.38.ra_ref), channel_id=1, source_target_pairs={{0,1},{1,0},{2,3},{3,2},{4,5},{5,4},{6,7},{7,6}} | collective-permute-start | bytes 28311560 | tf_op jit(solution)/shard_map/cond/branch_7_fun/ppermute | solution.py:217
  1095.8 14.6 %copy-start.19 = (s32[28672]{0:T(1024)}, s32[28672]{0:T(1024)S(1)}, u32[]{:S(2)}) copy-start(s32[28672]{0:T(1024)S(1)} %pad_add_fusion.7.dest_ref) | copy-start | bytes 344068 | tf_op jit(solution)/shard_map/cond

commit v2 on v0

v2 whole, which is shorter than its diff:
```python
import functools

import jax
import jax.numpy as jnp
from jax import lax
from jax.experimental import pallas as pl
from jax.experimental.pallas import tpu as pltpu
from jax.sharding import PartitionSpec as P

LANES = 128
ROW = 8
BLOCK = 512
WINDOW = BLOCK // 2 + 16
FAR = 1 << 20
VMEM = 61 * 2**20
FF_CHUNK = 768


def one_hot(index, size):
    return index[..., None] == jnp.arange(size, dtype=index.dtype)


def bdot(spec, a, b):
    return jnp.einsum(spec, a.astype(jnp.bfloat16), b.astype(jnp.bfloat16), preferred_element_type=jnp.float32)


def exclusive_rank(flags):
    rows, cols = flags.shape
    f = flags.astype(jnp.float32)
    before = jnp.arange(cols)[:, None] < jnp.arange(cols)[None, :]
    inside = bdot("hl,lm->hm", f, before)
    row_sum = f.sum(1)
    above = jnp.arange(rows)[:, None] < jnp.arange(rows)[None, :]
    offset = bdot("h,hm->m", row_sum, above)
    return (inside + offset[:, None]).astype(jnp.int32), row_sum.sum().astype(jnp.int32)


def invert(flags, rank, value, size):
    high = (one_hot(rank // LANES, size // LANES) & flags[:, None]).astype(jnp.bfloat16)
    low = one_hot(rank % LANES, LANES)
    vh = jnp.where(low, (value // LANES)[:, None], 0)
    vl = jnp.where(low, (value % LANES)[:, None], 0)
    th = bdot("kh,kl->hl", high, vh)
    tl = bdot("kh,kl->hl", high, vl)
    return (th * LANES + tl).astype(jnp.int32).reshape(size)


def lookup(table, index):
    high = one_hot(index // LANES, table.shape[0]).astype(jnp.bfloat16)
    low = one_hot(index % LANES, LANES)
    th = bdot("kh,hl->kl", high, table // LANES)
    tl = bdot("kh,hl->kl", high, table % LANES)
    return jnp.where(low, th * LANES + tl, 0).sum(1).astype(jnp.int32)


def params(**kw):
    return pltpu.CompilerParams(dimension_semantics=("arbitrary",), vmem_limit_bytes=VMEM, **kw)


def cost(flops, size):
    return pl.CostEstimate(flops=int(flops), bytes_accessed=int(size), transcendentals=0)


def blocks_of(rows):
    return -(-rows // BLOCK)


def phases(counts):
    first = [0]
    for c in counts:
        first.append(first[-1] + c)
    return first


def split_rows(ref, rows, base):
    for k in range(ref.shape[1] // LANES):
        rows[pl.ds(base + k, BLOCK, stride=ROW), :] = ref[:, k * LANES:(k + 1) * LANES].astype(jnp.float32)


def join_rows(rows, base, ref):
    for k in range(ref.shape[1] // LANES):
        ref[:, k * LANES:(k + 1) * LANES] = rows[pl.ds(base + k, BLOCK, stride=ROW), :].astype(ref.dtype)


def line(r):
    return pl.ds(pl.multiple_of(r * ROW, ROW), ROW)


def compact_kernel(first, last, base_ref, pos_ref, *refs):
    parts, out_ref, acc = refs[:-2], refs[-2], refs[-1]
    i = pl.program_id(0)
    d = out_ref.shape[1]

    @pl.when(i == 0)
    def _():
        acc[...] = jnp.zeros_like(acc)

    base = pl.multiple_of(base_ref[i], 16)
    spots = lax.broadcasted_iota(jnp.int32, (WINDOW, BLOCK), 0) + base
    pick = jnp.where(spots == pos_ref[0], 1.0, 0.0).astype(jnp.bfloat16)
    for lo, hi, ref in zip(first[:-1], first[1:], parts):
        @pl.when((i >= lo) & (i < hi))
        def _(ref=ref):
            moved = jnp.dot(pick, ref[...], preferred_element_type=jnp.float32)
            acc[pl.ds(base, WINDOW), :] = acc[pl.ds(base, WINDOW), :] + moved

    @pl.when(i == last)
    def _():
        out_ref[...] = acc[0:out_ref.shape[0], :].astype(out_ref.dtype)


def compact(parts, pos, rows):
    d = parts[0].shape[1]
    counts = [p.shape[0] // BLOCK for p in parts]
    first = phases(counts)
    pos = pos.reshape(-1, BLOCK)
    low = jnp.where(pos >= 0, pos, FAR).min(1)
    base = jnp.where(low < FAR, jnp.minimum(low, rows) // 16 * 16, 0)

    def spec(k):
        return pl.BlockSpec((BLOCK, d), lambda i, *_: (jnp.clip(i - first[k], 0, counts[k] - 1), 0))

    return pl.pallas_call(
        functools.partial(compact_kernel, first, first[-1] - 1),
        grid_spec=pltpu.PrefetchScalarGridSpec(
            num_scalar_prefetch=1,
            grid=(first[-1],),
            in_specs=[pl.BlockSpec((1, 1, BLOCK), lambda i, *_: (i, 0, 0))] + [spec(k) for k in range(len(parts))],
            out_specs=pl.BlockSpec((rows, d), lambda i, *_: (0, 0)),
            scratch_shapes=[pltpu.VMEM((rows + WINDOW, d), jnp.float32)],
        ),
        out_shape=jax.ShapeDtypeStruct((rows, d), parts[0].dtype),
        compiler_params=params(),
        cost_estimate=cost(2e10, 2 * d * (sum(p.shape[0] for p in parts) + rows)),
        name="compact",
    )(base, pos[:, None, :], *parts)


def gather_kernel(first, stride, has_init, pos_ref, slot_ref, start_ref, *refs):
    refs, out_ref, acc, rows = refs[:-3], refs[-3], refs[-2], refs[-1]
    i = pl.program_id(0)
    if has_init:
        @pl.when(i < first[1])
        def _():
            split_rows(refs[0], acc, i * BLOCK * ROW)
        refs, first = refs[1:], first[1:]
    else:
        @pl.when(i == 0)
        def _():
            acc[...] = jnp.zeros_like(acc)

    for p, ref in enumerate(refs):
        @pl.when((i >= first[p]) & (i < first[p + 1]))
        def _(p=p, ref=ref):
            split_rows(ref, rows, 0)
            v = p * stride + i - first[p]
            low = v * BLOCK
            start, end = start_ref[v], start_ref[v + 1]
            full = (end - start) // 8

            def eight(j, c):
                at = start + j * 8
                values = [rows[line(pos_ref[at + u] - low), :] for u in range(8)]
                for u in range(8):
                    acc[line(slot_ref[at + u]), :] = values[u]
                return c

            def single(j, c):
                acc[line(slot_ref[j]), :] = rows[line(pos_ref[j] - low), :]
                return c

            lax.fori_loop(0, full, eight, 0)
            lax.fori_loop(start + full * 8, end, single, 0)

    @pl.when(i >= first[len(refs)])
    def _():
        join_rows(acc, (i - first[len(refs)]) * BLOCK * ROW, out_ref)


def gather(init, part_rows, parts, key, slots, stride):
    d = parts[0].shape[1]
    counts = [blocks_of(p.shape[0]) for p in parts]
    has_init = init is not None
    ins = list(parts)
    if has_init:
        counts, ins = [slots // BLOCK] + counts, [init[0]] + ins
    counts = counts + [slots // BLOCK]
    first = phases(counts)
    key, slot = lax.sort((key, jnp.arange(slots, dtype=jnp.int32)), num_keys=1)
    edges = jnp.arange(len(parts) * stride + 1, dtype=jnp.int32) * BLOCK
    starts = (key[None, :] < edges[:, None]).sum(1).astype(jnp.int32)

    def spec(k, off=0):
        return pl.BlockSpec((BLOCK, d), lambda i, *_: (jnp.clip(i - first[k], 0, counts[k] - 1) + off, 0))

    offs = [init[1] if has_init else 0] + [0] * len(parts)
    return pl.pallas_call(
        functools.partial(gather_kernel, first, stride, has_init),
        grid_spec=pltpu.PrefetchScalarGridSpec(
            num_scalar_prefetch=3,
            grid=(first[-1],),
            in_specs=[spec(k, offs[k]) for k in range(len(ins))],
            out_specs=spec(len(counts) - 1),
            scratch_shapes=[pltpu.VMEM((slots * ROW, LANES), jnp.float32), pltpu.VMEM((BLOCK * ROW, LANES), jnp.float32)],
        ),
        out_shape=jax.ShapeDtypeStruct((slots, d), parts[0].dtype),
        compiler_params=params(),
        cost_estimate=cost(4e10, 2 * d * (sum(p.shape[0] for p in ins) + slots)),
        name="gather",
    )(key, slot, starts, *ins)


def ffn_kernel(x_ref, w_in_ref, w_out_ref, gate_ref, out_ref):
    f = w_in_ref.shape[2]
    x = x_ref[...]
    total = None
    for lo in range(0, f, FF_CHUNK):
        pre = jnp.dot(x, w_in_ref[0, :, lo:lo + FF_CHUNK], preferred_element_type=jnp.float32)
        hidden = jax.nn.gelu(pre, approximate=True).astype(jnp.bfloat16)
        part = jnp.dot(hidden, w_out_ref[0, lo:lo + FF_CHUNK, :], preferred_element_type=jnp.float32)
        total = part if total is None else total + part
    out_ref[...] = (gate_ref[0] * total).astype(out_ref.dtype)


def ffn(x, w_in, w_out, gate, turn, turns):
    count, cap = gate.shape[0], gate.shape[1]
    d, f = w_in.shape[1], w_in.shape[2]
    return pl.pallas_call(
        ffn_kernel,
        grid=(count,),
        in_specs=[
            pl.BlockSpec((cap, d), lambda i: (i, 0)),
            pl.BlockSpec((1, d, f), lambda i: (i * turns + turn, 0, 0)),
            pl.BlockSpec((1, f, d), lambda i: (i * turns + turn, 0, 0)),
            pl.BlockSpec((1, cap, 1), lambda i: (i, 0, 0)),
        ],
        out_specs=pl.BlockSpec((cap, d), lambda i: (i, 0)),
        out_shape=jax.ShapeDtypeStruct((count * cap, d), x.dtype),
        compiler_params=params(),
        cost_estimate=cost(4 * count * cap * d * f, 4 * count * d * f),
        name="ffn",
    )(x, w_in, w_out, gate)


def combine_kernel(first, dest_ref, dup_ref, tok_ref, *refs):
    parts, out_ref, acc, rows = refs[:-3], refs[-3], refs[-2], refs[-1]
    i = pl.program_id(0)

    @pl.when(i < first[1])
    def _():
        split_rows(tok_ref, acc, i * BLOCK * ROW)

    for p, ref in enumerate(parts):
        @pl.when((i >= first[p + 1]) & (i < first[p + 2]))
        def _(ref=ref):
            step = i - first[1]
            start = step * BLOCK
            split_rows(ref, rows, 0)

            @pl.when(dup_ref[step] == 0)
            def _():
                def body(j, c):
                    where = [line(dest_ref[start + j * 8 + u]) for u in range(8)]
                    sums = [acc[where[u], :] + rows[line(j * 8 + u), :] for u in range(8)]
                    for u in range(8):
                        acc[where[u], :] = sums[u]
                    return c
                lax.fori_loop(0, BLOCK // 8, body, 0)

            @pl.when(dup_ref[step] != 0)
            def _():
                def body(r, c):
                    w = line(dest_ref[start + r])
                    acc[w, :] = acc[w, :] + rows[line(r), :]
                    return c
                lax.fori_loop(0, BLOCK, body, 0)

    @pl.when(i >= first[-2])
    def _():
        join_rows(acc, (i - first[-2]) * BLOCK * ROW, out_ref)


def combine(init, parts, dests, dtype):
    n, d = init.shape
    counts = [n // BLOCK] + [blocks_of(p.shape[0]) for p in parts] + [n // BLOCK]
    first = phases(counts)
    dest = jnp.concatenate([jnp.pad(x[:p.shape[0]], (0, -p.shape[0] % BLOCK), constant_values=n) for p, x in zip(parts, dests)])
    groups = dest.reshape(-1, 8)
    same = jnp.zeros(groups.shape[:1], bool)
    for u in range(1, 8):
        same |= ((groups[:, u:] == groups[:, :-u]) & (groups[:, u:] < n)).any(1)
    dup = same.reshape(-1, BLOCK // 8).any(1).astype(jnp.int32)

    def spec(k):
        return pl.BlockSpec((BLOCK, d), lambda i, *_: (jnp.clip(i - first[k], 0, counts[k] - 1), 0))

    return pl.pallas_call(
        functools.partial(combine_kernel, first),
        grid_spec=pltpu.PrefetchScalarGridSpec(
            num_scalar_prefetch=2,
            grid=(first[-1],),
            in_specs=[spec(k) for k in range(len(parts) + 1)],
            out_specs=spec(len(parts) + 1),
            scratch_shapes=[pltpu.VMEM(((n + 1) * ROW, LANES), jnp.float32), pltpu.VMEM((BLOCK * ROW, LANES), jnp.float32)],
        ),
        out_shape=jax.ShapeDtypeStruct((n, d), dtype),
        compiler_params=params(),
        cost_estimate=cost(1e11, 2 * d * dest.shape[0]),
        name="combine",
    )(dest, dup, init, *parts)


def solution(mesh):
    group_n = mesh.shape["ep"]
    row_spec = P(("dp", "ep"), None)
    expert_spec = P("ep", None, None)
    swap_core = [(g, g ^ 1) for g in range(group_n)]
    swap_chip = [(g, g ^ 2) for g in range(group_n)]

    def local_layer(tok_loc, sel_loc, gate_loc, win_loc, wout_loc):
        n, d = tok_loc.shape
        exp_count, cap_slots = sel_loc.shape
        turns = 2
        experts = exp_count // turns
        part = experts * cap_slots
        me = lax.axis_index("ep")
        chip, core = me // 2, me % 2
        chip_n = 2 * n
        levels = [(min(part, -(-(L * 15 // 16) // 128) * 128), min(part, -(-(L * 13 // 16) // 128) * 128), L) for L in range(2048, part, 256)]
        levels.append((part, part, part))

        def by_turn(x):
            return jnp.swapaxes(x.reshape(x.shape[:-2] + (experts, turns, cap_slots)), -3, -2).reshape(x.shape[:-2] + (turns, part))

        sib_tok = lax.ppermute(tok_loc, "ep", swap_core)
        mine = by_turn(sel_loc)
        all_sel = lax.all_gather(mine, "ep").reshape(2, 2, turns, part)
        chip_sel = lax.dynamic_index_in_dim(all_sel, chip, 0, keepdims=False)
        far_sel = lax.dynamic_index_in_dim(all_sel, 1 - chip, 0, keepdims=False)
        sib = lax.dynamic_index_in_dim(chip_sel, 1 - core, 0, keepdims=False)

        def needed(sel, owner):
            idx = sel.reshape(-1) - owner * chip_n
            high = one_hot(idx // LANES, chip_n // LANES)
            return bdot("kh,kl->hl", high, one_hot(idx % LANES, LANES)) > 0

        def news(sel, owner):
            a, b = needed(sel[:, 0], owner), needed(sel[:, 1], owner)
            return [a, b & ~a]

        give, want = news(far_sel, chip), news(chip_sel, 1 - chip)
        give_rank, give_n = zip(*[exclusive_rank(x) for x in give])
        want_rank, want_n = zip(*[exclusive_rank(x) for x in want])
        back_far = [chip_sel[:, h].reshape(-1) // chip_n != chip for h in range(turns)]
        come_far = [far_sel[:, h].reshape(-1) // chip_n == chip for h in range(turns)]
        back_rank, back_n = zip(*[exclusive_rank(x.reshape(-1, LANES)) for x in back_far])
        come_rank, come_n = zip(*[exclusive_rank(x.reshape(-1, LANES)) for x in come_far])
        most = jnp.stack([jnp.maximum(give_n[0], want_n[0]), jnp.maximum(give_n[1], want_n[1]),
                          jnp.maximum(jnp.maximum(back_n[0], come_n[0]), jnp.maximum(back_n[1], come_n[1]))])
        caps = 2 * jnp.array(levels, jnp.int32)
        level = (caps[:-1] < most[None, :]).any(1).sum().astype(jnp.int32)
        level = lax.pmax(level, ("dp", "ep"))

        def my_turn(flags, rank):
            flags, rank = flags.reshape(-1), rank.reshape(-1)
            pos = jnp.where(flags & (rank % 2 == core), rank // 2, -1).reshape(2, -1)
            return jnp.where(core == 0, pos, pos[::-1]).reshape(-1)

        give_pos = [my_turn(give[h], give_rank[h]) for h in range(turns)]

        def place(v):
            return jnp.where((v >= 0) & (v < n), v, n)

        def run_level(rows):
            def run(tok, sib_tok, give_pos, want, want_rank, mine, sib, far_sel, back_far, back_rank, come_far, come_rank, come_n, gate, w_in, w_out):
                sent = [compact([tok, sib_tok], give_pos[h], rows[h]) for h in range(turns)]
                got = [lax.ppermute(x, "ep", swap_chip) for x in sent]
                sib_got = [lax.ppermute(x, "ep", swap_core) for x in got]

                near_key = jnp.where(mine // chip_n == chip, (mine - me * n) % chip_n, FAR).reshape(-1)
                x_near = gather(None, n, [tok, sib_tok], near_key, turns * part, n // BLOCK)
                code = jnp.where(want[0], want_rank[0], want_rank[1] + 2 * part)
                lists, x, p = [], [], []
                for h in range(turns):
                    is_far = mine[h] // chip_n != chip
                    c = lookup(code, mine[h] - (1 - chip) * chip_n)
                    late, rank = c // (2 * part), c % (2 * part)
                    key = (late * 2 + jnp.where(rank % 2 == core, 0, 1)) * part + rank // 2
                    key = jnp.where(is_far, key, FAR)
                    tables = [t for k in range(h + 1) for t in (got[k], sib_got[k])]
                    x.append(gather((x_near, h * (part // BLOCK)), part, tables, key, part, part // BLOCK))
                    p.append(ffn(x[h], w_in, w_out, gate[h], h, turns))
                sib_p = [lax.ppermute(y, "ep", swap_core) for y in p]
                back = [compact([p[h], sib_p[h]], my_turn(back_far[h], back_rank[h]), rows[2]) for h in range(turns)]
                back_got = [lax.ppermute(y, "ep", swap_chip) for y in back]
                sib_back = [lax.ppermute(y, "ep", swap_core) for y in back_got]
                ids = jnp.arange(2 * part, dtype=jnp.int32)
                come = []
                for h in range(turns):
                    t = far_sel[:, h].reshape(-1) - chip * chip_n
                    t = invert(come_far[h], come_rank[h].reshape(-1), jnp.clip(t, 0, chip_n - 1), 2 * part)
                    t = place(jnp.where(ids < come_n[h], t - core * n, n)).reshape(-1, 2)
                    come.append([lax.dynamic_index_in_dim(t, k, 1, keepdims=False) for k in (core, 1 - core)])
                own_to = [place(mine[h] - me * n) for h in range(turns)]
                sib_to = [place(sib[h] - me * n) for h in range(turns)]
                acc = combine(tok, [p[0], p[1], sib_p[0], sib_p[1], back_got[0], sib_back[0]],
                              [own_to[0], own_to[1], sib_to[0], sib_to[1]] + come[0], jnp.float32)
                return combine(acc, [back_got[1], sib_back[1]], come[1], tok.dtype)
            return run

        gate = jnp.swapaxes(gate_loc.reshape(experts, turns, cap_slots), 0, 1)[..., None]
        return lax.switch(level, [run_level(r) for r in levels], tok_loc, sib_tok, give_pos, want, want_rank, mine, sib, far_sel,
                          back_far, back_rank, come_far, come_rank, come_n, gate, win_loc, wout_loc)

    return jax.shard_map(local_layer, mesh=mesh, in_specs=(row_spec, row_spec, row_spec, expert_spec, expert_spec), out_specs=row_spec, check_vma=False)
```

time: 1330 us -> 941 us (0.71)
  Pallas kernels: 0 us -> 490 us
  local copies, waits for them, and re-layouts: 421 us -> 34.1 us
  waiting for transfers between devices: 530 us -> 242 us
  other arithmetic: 250 us -> 43.3 us
  matrix products: 107 us -> 35.4 us
  blocking collectives: 8.53 us -> 55.4 us
  loops' own time: 0 us -> 35 us
    all_to_all x2 -> x0, waiting for transfers between devices: 530 us -> none  [the longest x1 272 us: local_layer(): got_rows = lax.all_to_all(send_rows, 'ep', 0, 0, tiled=True)]
    pallas_call x0 -> x11, Pallas kernels: none -> 490 us  [the longest x2 157 us: combine(): pl.pallas_call(functools.partial(combine_kernel, first), grid_spec=pltpu....]
    gather x6 -> x0, local copies, waits for them, and re-layouts: 389 us -> none  [the longest x1 90.5 us: local_layer(): slot_order[jnp.minimum(starts[:, None] + lane_idx[None, :], slot_total - 1)]]
    ppermute x0 -> x11, waiting for transfers between devices: none -> 242 us  [the longest x2 164 us: run(): back_got = [lax.ppermute(y, 'ep', swap_chip) for y in back]]
    scatter-add x2 -> x0, other arithmetic: 189 us -> none  [the longest x1 132 us: local_layer(): jax.ops.segment_sum(returned.reshape(group_n * pair_cap, model_dim).astyp...]
    dot_general x1 -> x28, matrix products: 107 us -> 35.4 us  [bdot(): jnp.einsum(spec, a.astype(jnp.bfloat16), b.astype(jnp.bfloat16), preferre...]
    another operation x0 -> x1, loops' own time: none -> 35 us  [local_layer(): lax.switch(level, [run_level(r) for r in levels], tok_loc, sib_tok, give_...]
    pmax x0 -> x1, blocking collectives: none -> 32.6 us  [local_layer(): level = lax.pmax(level, ('dp', 'ep'))]
  transfers between devices with their start and end apart: 2 -> 11, of which waited for: 2 -> 4; matrix products, arithmetic and copies ran while one was open for 1% -> 12% of each run, Pallas kernels for 0% -> 43%
where the time goes in v2:
time: 941 us; the launch traced here: 957 us
  Pallas kernels  490 us (52%)
  waiting for transfers between devices  242 us (26%)
  blocking collectives  55.4 us (6%)
  other arithmetic  43.3 us (5%)
  matrix products  35.4 us (4%)
  loops' own time  35 us (4%)
  local copies, waits for them, and re-layouts  34.1 us (4%)
  starting transfers between devices  13.7 us (1%)
    ppermute x2, waiting for transfers between devices, run(): back_got = [lax.ppermute(y, 'ep', swap_chip) for y in back]  164 us
    pallas_call x2, Pallas kernels, combine(): pl.pallas_call(functools.partial(combine_kernel, first), grid_spec=pltpu....  157 us
    pallas_call x2, Pallas kernels, ffn(): pl.pallas_call(ffn_kernel, grid=(count,), in_specs=[pl.BlockSpec((cap, d)...  121 us
    pallas_call x3, Pallas kernels, gather(): pl.pallas_call(functools.partial(gather_kernel, first, stride, has_init),...  115 us
    pallas_call x4, Pallas kernels, compact(): pl.pallas_call(functools.partial(compact_kernel, first, first[-1] - 1), g...  96.7 us
    ppermute x2, waiting for transfers between devices, run(): got = [lax.ppermute(x, 'ep', swap_chip) for x in sent]  78.3 us
    dot_general x28, matrix products, bdot(): jnp.einsum(spec, a.astype(jnp.bfloat16), b.astype(jnp.bfloat16), preferre...  35.4 us
    another operation x1, loops' own time, local_layer(): lax.switch(level, [run_level(r) for r in levels], tok_loc, sib_tok, give_...  35 us
  transfers between devices with their start and end apart: 11, of which 4 were waited for; matrix products, arithmetic and copies ran while one was open for 12% of the time, Pallas kernels for 43%

profile of v2, /device:TPU:0, one launch (start us, length us, event | category | flops | bytes accessed | tf_op | source)
XLA Modules:
  0.0 956.8 jit_solution(6662845600020357526)
XLA Ops:
  1.7 22.8 %all_gather.3 = s32[4,2,4096]{2,1,0:T(2,128)S(1)} all-gather(s32[1,2,4096]{2,1,0:T(2,128)S(1)} %bitcast.1015), channel_id=1, replica_groups=mesh['dp'=2,'ep'=4] {'ep'}, dimensions={0}, use_global_device_ids=true | all-gather | bytes 163840 | tf_op jit(solution)/shard_map/all_gather | solution.py:337
  29.3 4.1 convert_reduce_fusion.31
  33.4 4.1 convert_reduce_fusion.27
  38.4 4.1 convert_reduce_fusion.29
  42.5 4.1 fusion.1694
  49.5 32.6 %pmax.7 = s32[]{:T(128)} all-reduce(s32[]{:T(128)} %convert_reduce_fusion.37), channel_id=1, replica_groups=mesh['dp'=2,'ep'=4] {'dp','ep'}, use_global_device_ids=true, to_apply=%region_10.11 | all-reduce | flops 1 | bytes 8 | tf_op jit(solution)/shard_map/pmax | solution.py:362
  92.1 863.4 %conditional.1 = (bf16[8192,768]{1,0:T(8,128)(2,1)}) conditional(s32[]{:T(128)} %clamp.173, (s32[]{:T(128)}, s32[64,128]{1,0:T(8,128)}, s32[8192]{0:T(1024)}, s32[2,2,4096]{2,1,0:T(2,128)}, s32[]{:T(128)}, /*index=5*/s32[]{:T(128)}, s32[2,16,256]{2,0,1:T(2,128)S(1)}, s32[]{:T(128)}, s32[2,2,2,4096]{3,2,1,0:T(2,128)}, ...), branch_computations={%region_19.46_spmd, %region_46.73_spmd, %region_73.100_spmd, %regi... | conditional | flops 478412570624 | bytes 837963392 | solution.py:412
  118.8 30.6 %compact.56 = bf16[3200,768]{1,0:T(8,128)(2,1)} custom-call(s32[32]{0:T(128)} %get-tuple-element.16520.base_ref, s32[32,1,512]{2,1,0:T(1,128)} %reshape_reshape.93.pos_ref, bf16[8192,768]{1,0:T(8,128)(2,1)} %get-tuple-element.655.refs_0_.tok_ref, bf16[8192,768]{1,0:T(8,128)(2,1)} %get-tuple-element.663.refs_1_), custom_call_target="tpu_custom_call" | custom-call | flops 20000000000 | bytes 30081024 | tf_op jit(solution)/shard_map/cond/branch_5_fun/compact/pallas_call | solution.py:123
  152.4 30.2 %compact.57 = bf16[2816,768]{1,0:T(8,128)(2,1)} custom-call(s32[32]{0:T(128)} %get-tuple-element.16519.base_ref, s32[32,1,512]{2,1,0:T(1,128)} %reshape_reshape.95.pos_ref, bf16[8192,768]{1,0:T(8,128)(2,1)} %get-tuple-element.655.refs_0_.tok_ref, bf16[8192,768]{1,0:T(8,128)(2,1)} %get-tuple-element.663.refs_1_), custom_call_target="tpu_custom_call" | custom-call | flops 20000000000 | bytes 29491200 | tf_op jit(solution)/shard_map/cond/branch_5_fun/compact/pallas_call | solution.py:123
  188.4 70.1 %collective-permute-done.50.refs_1_ = bf16[3200,768]{1,0:T(8,128)(2,1)} collective-permute-done((bf16[3200,768]{1,0:T(8,128)(2,1)}, bf16[3200,768]{1,0:T(8,128)(2,1)}, u32[]{:S(2)}, u32[]{:S(2)}) %collective-permute-start.50) | collective-permute-done | bytes 4915232 | tf_op jit(solution)/shard_map/cond/branch_5_fun/ppermute | solution.py:377
  262.5 9.5 rev.50
  271.9 5.8 sort.393
  277.7 6.8 sort.394
  285.9 5.8 sort.395
  294.2 47.4 %gather.42.refs_0_ = bf16[8192,768]{1,0:T(8,128)(2,1)} custom-call(s32[8192]{0:T(1024)} %copy-done.235, s32[8192]{0:T(1024)} %get-tuple-element.662.slot_ref, s32[33]{0:T(128)} %convert_reduce_fusion.15.start_ref, bf16[8192,768]{1,0:T(8,128)(2,1)} %get-tuple-element.655.refs_0_.tok_ref, bf16[8192,768]{1,0:T(8,128)(2,1)} %get-tuple-element.663.refs_1_), custom_call_target="tpu_custom_call" | custom-call | flops 40000000000 | bytes 37748736 | tf_op jit(solution)/shard_map/cond/branch_5_fun/gather/pallas_call | solution.py:197
  341.6 8.2 collective-permute-done.52.refs_3_
  349.8 28.4 %gather.43.x_ref = bf16[4096,768]{1,0:T(8,128)(2,1)} custom-call(s32[4096]{0:T(1024)} %copy-done.249, s32[4096]{0:T(1024)} %get-tuple-element.660.slot_ref, s32[17]{0:T(128)} %convert_reduce_fusion.17.start_ref, bf16[8192,768]{1,0:T(8,128)(2,1)} %gather.42.refs_0_, bf16[3200,768]{1,0:T(8,128)(2,1)} %collective-permute-done.50.refs_1_, ...), custom_call_target="tpu_custom_call" | custom-call | flops 40000000000 | bytes 28704768 | tf_op jit(solution)/shard_map/cond/branch_5_fun/gather/pallas_call | solution.py:197
  378.2 60.6 %ffn.28.refs_0_ = bf16[4096,768]{1,0:T(8,128)(2,1)} custom-call(bf16[4096,768]{1,0:T(8,128)(2,1)} %gather.43.x_ref, bf16[32,768,3072]{2,1,0:T(8,128)(2,1)} %get-tuple-element.1038.w_in_ref, bf16[32,3072,768]{2,1,0:T(8,128)(2,1)} %get-tuple-element.1047.w_out_ref, f32[16,256,1]{2,1,0:T(8,128)} %copy.1498.gate_ref), custom_call_target="tpu_custom_call" | custom-call | flops 38654705664 | bytes 150994944 | tf_op jit(solution)/shard_map/cond/branch_5_fun/ffn/pallas_call | solution.py:228
  438.8 4.2 collective-permute-start.54
  443.0 39.4 %gather.44.x_ref = bf16[4096,768]{1,0:T(8,128)(2,1)} custom-call(s32[4096]{0:T(1024)} %copy-done.252, s32[4096]{0:T(1024)} %get-tuple-element.669.slot_ref, s32[33]{0:T(128)} %convert_reduce_fusion.16.start_ref, bf16[8192,768]{1,0:T(8,128)(2,1)} %gather.42.refs_0_, bf16[3200,768]{1,0:T(8,128)(2,1)} %collective-permute-done.50.refs_1_, ...), custom_call_target="tpu_custom_call" | custom-call | flops 40000000000 | bytes 37355520 | tf_op jit(solution)/shard_map/cond/branch_5_fun/gather/pallas_call | solution.py:197
  482.4 60.8 %ffn.29.refs_1_.refs_0_ = bf16[4096,768]{1,0:T(8,128)(2,1)} custom-call(bf16[4096,768]{1,0:T(8,128)(2,1)} %gather.44.x_ref, bf16[32,768,3072]{2,1,0:T(8,128)(2,1)} %get-tuple-element.1038.w_in_ref, bf16[32,3072,768]{2,1,0:T(8,128)(2,1)} %get-tuple-element.1047.w_out_ref, f32[16,256,1]{2,1,0:T(8,128)} %copy.1499.gate_ref), custom_call_target="tpu_custom_call" | custom-call | flops 38654705664 | bytes 150994944 | tf_op jit(solution)/shard_map/cond/branch_5_fun/ffn/pallas_call | solution.py:228
  543.1 4.3 collective-permute-start.55
  549.8 17.8 %compact.58 = bf16[3328,768]{1,0:T(8,128)(2,1)} custom-call(s32[16]{0:T(128)} %compare_select_fusion.123.base_ref, s32[16,1,512]{2,1,0:T(1,128)} %reshape.3706.pos_ref, bf16[4096,768]{1,0:T(8,128)(2,1)} %ffn.28.refs_0_, bf16[4096,768]{1,0:T(8,128)(2,1)} %collective-permute-done.54.refs_1_.refs_2_), custom_call_target="tpu_custom_call" | custom-call | flops 20000000000 | bytes 17694720 | tf_op jit(solution)/shard_map/cond/branch_5_fun/compact/pallas_call | solution.py:123
  571.9 2.4 fusion.960
  574.3 18.1 %compact.59 = bf16[3328,768]{1,0:T(8,128)(2,1)} custom-call(s32[16]{0:T(128)} %compare_select_fusion.122.base_ref, s32[16,1,512]{2,1,0:T(1,128)} %reshape.3710.pos_ref, bf16[4096,768]{1,0:T(8,128)(2,1)} %ffn.29.refs_1_.refs_0_, bf16[4096,768]{1,0:T(8,128)(2,1)} %collective-permute-done.55.refs_3_.refs_1_), custom_call_target="tpu_custom_call" | custom-call | flops 20000000000 | bytes 17694720 | tf_op jit(solution)/shard_map/cond/branch_5_fun/compact/pallas_call | solution.py:123
  594.4 86.3 %collective-permute-done.56.refs_4_ = bf16[3328,768]{1,0:T(8,128)(2,1)} collective-permute-done((bf16[3328,768]{1,0:T(8,128)(2,1)}, bf16[3328,768]{1,0:T(8,128)(2,1)}, u32[]{:S(2)}, u32[]{:S(2)}) %collective-permute-start.56) | collective-permute-done | bytes 5111840 | tf_op jit(solution)/shard_map/cond/branch_5_fun/ppermute | solution.py:395
  680.8 3.5 sub.1669
  689.0 3.5 sub.1655
  692.5 3.2 and_select_fusion.40
  711.7 77.7 %collective-permute-done.58.refs_0_ = bf16[3328,768]{1,0:T(8,128)(2,1)} collective-permute-done((bf16[3328,768]{1,0:T(8,128)(2,1)}, bf16[3328,768]{1,0:T(8,128)(2,1)}, u32[]{:S(2)}, u32[]{:S(2)}) %collective-permute-start.58) | collective-permute-done | bytes 5111840 | tf_op jit(solution)/shard_map/cond/branch_5_fun/ppermute | solution.py:395
  789.4 106.8 %combine.28.tok_ref = f32[8192,768]{1,0:T(8,128)} custom-call(s32[23552]{0:T(1024)} %copy-done.206, s32[46]{0:T(128)} %convert_element_type.539.dup_ref, bf16[8192,768]{1,0:T(8,128)(2,1)} %get-tuple-element.655.refs_0_.tok_ref, bf16[4096,768]{1,0:T(8,128)(2,1)} %ffn.28.refs_0_, bf16[4096,768]{1,0:T(8,128)(2,1)} %ffn.29.refs_1_.refs_0_, ...), custom_call_target="tpu_custom_call" | custom-call | flops 99999997952 | bytes 36175872 | tf_op jit(solution)/shard_map/cond/branch_5_fun/combine/pallas_call | solution.py:297
  896.1 50.0 %combine.29 = bf16[8192,768]{1,0:T(8,128)(2,1)} custom-call(s32[7168]{0:T(1024)} %pad_add_fusion.10.dest_ref, s32[14]{0:T(128)} %convert_element_type.535.dup_ref, f32[8192,768]{1,0:T(8,128)} %combine.28.tok_ref, bf16[3328,768]{1,0:T(8,128)(2,1)} %collective-permute-done.58.refs_0_, bf16[3328,768]{1,0:T(8,128)(2,1)} %collective-permute-done.59.refs_1_), custom_call_target="tpu_custom_call" | custom-call | flops 99999997952 | bytes 11010048 | tf_op jit(solution)/shard_map/cond/branch_5_fun/combine/pallas_call | solution.py:297
  (230 shorter events, 61.2 us)
Async XLA Ops:
  0.0 92.0 %collective-permute-start.90 = (bf16[8192,768]{1,0:T(8,128)(2,1)}, bf16[8192,768]{1,0:T(8,128)(2,1)}, u32[]{:S(2)}, u32[]{:S(2)}) collective-permute-start(bf16[8192,768]{1,0:T(8,128)(2,1)} %param.15), channel_id=1, source_target_pairs={{0,1},{1,0},{2,3},{3,2},{4,5},{5,4},{6,7},{7,6}} | collective-permute-start | bytes 37748744 | tf_op jit(solution)/shard_map/ppermute | solution.py:335
  28.6 61.7 %copy-start.128 = (s32[2,1,4096]{2,1,0:T(1,128)}, s32[2,1,4096]{2,1,0:T(1,128)S(1)}, u32[]{:S(2)}) copy-start(s32[2,1,4096]{2,1,0:T(1,128)S(1)} %get-tuple-element.16644) | copy-start | bytes 98308
  28.6 62.4 %copy-start.118 = (s32[2,1,4096]{2,1,0:T(1,128)}, s32[2,1,4096]{2,1,0:T(1,128)S(1)}, u32[]{:S(2)}) copy-start(s32[2,1,4096]{2,1,0:T(1,128)S(1)} %get-tuple-element.16643) | copy-start | bytes 98308
  42.5 39.7 %copy-start.229 = (f32[32,256]{1,0:T(8,128)S(1)}, f32[32,256]{1,0:T(8,128)}, u32[]{:S(2)}) copy-start(f32[32,256]{1,0:T(8,128)} %param.17) | copy-start | bytes 98308
  117.0 69.0 %copy-start.10 = (s32[8192]{0:T(1024)}, s32[8192]{0:T(1024)S(1)}, u32[]{:S(2)}) copy-start(s32[8192]{0:T(1024)S(1)} %get-tuple-element.16700) | copy-start | bytes 98308 | tf_op jit(solution)/shard_map/cond
  117.0 69.0 %copy-start.28 = (s32[8192]{0:T(1024)}, s32[8192]{0:T(1024)S(1)}, u32[]{:S(2)}) copy-start(s32[8192]{0:T(1024)S(1)} %get-tuple-element.16709) | copy-start | bytes 98308 | tf_op jit(solution)/shard_map/cond
  117.0 69.0 %copy-start.46 = (s32[8192]{0:T(1024)}, s32[8192]{0:T(1024)S(1)}, u32[]{:S(2)}) copy-start(s32[8192]{0:T(1024)S(1)} %get-tuple-element.16718) | copy-start | bytes 98308 | tf_op jit(solution)/shard_map/cond
  117.0 69.0 %copy-start.64 = (s32[8192]{0:T(1024)}, s32[8192]{0:T(1024)S(1)}, u32[]{:S(2)}) copy-start(s32[8192]{0:T(1024)S(1)} %get-tuple-element.16727) | copy-start | bytes 98308 | tf_op jit(solution)/shard_map/cond
  149.4 109.1 %collective-permute-start.50 = (bf16[3200,768]{1,0:T(8,128)(2,1)}, bf16[3200,768]{1,0:T(8,128)(2,1)}, u32[]{:S(2)}, u32[]{:S(2)}) collective-permute-start(bf16[3200,768]{1,0:T(8,128)(2,1)} %compact.56), channel_id=1, source_target_pairs={{0,2},{1,3},{2,0},{3,1},{4,6},{5,7},{6,4},{7,5}} | collective-permute-start | bytes 14745608 | tf_op jit(solution)/shard_map/cond/branch_5_fun/ppermute | solution.py:377
  182.6 167.2 %collective-permute-start.52 = (bf16[2816,768]{1,0:T(8,128)(2,1)}, bf16[2816,768]{1,0:T(8,128)(2,1)}, u32[]{:S(2)}, u32[]{:S(2)}) collective-permute-start(bf16[2816,768]{1,0:T(8,128)(2,1)} %compact.57), channel_id=1, source_target_pairs={{0,2},{1,3},{2,0},{3,1},{4,6},{5,7},{6,4},{7,5}} | collective-permute-start | bytes 12976136 | tf_op jit(solution)/shard_map/cond/branch_5_fun/ppermute | solution.py:377
  258.5 91.2 %collective-permute-start.51 = (bf16[3200,768]{1,0:T(8,128)(2,1)}, bf16[3200,768]{1,0:T(8,128)(2,1)}, u32[]{:S(2)}, u32[]{:S(2)}) collective-permute-start(bf16[3200,768]{1,0:T(8,128)(2,1)} %collective-permute-done.50.refs_1_), channel_id=1, source_target_pairs={{0,1},{1,0},{2,3},{3,2},{4,5},{5,4},{6,7},{7,6}} | collective-permute-start | bytes 14745608 | tf_op jit(solution)/shard_map/cond/branch_5_fun/ppermute | solution.py:378
  262.5 79.1 %copy-start.183 = (s32[2,4096]{1,0:T(2,128)}, s32[2,4096]{1,0:T(2,128)S(1)}, u32[]{:S(2)}) copy-start(s32[2,4096]{1,0:T(2,128)S(1)} %reshape.3704) | copy-start | bytes 98308 | tf_op jit(solution)/shard_map/cond
  277.7 63.8 %copy-start.249 = (s32[4096]{0:T(1024)}, s32[4096]{0:T(1024)S(1)}, u32[]{:S(2)}) copy-start(s32[4096]{0:T(1024)S(1)} %get-tuple-element.659.pos_ref) | copy-start | bytes 49156 | tf_op jit(solution)/shard_map/cond
  285.9 55.7 %copy-start.204 = (s32[23552]{0:T(1024)}, s32[23552]{0:T(1024)S(1)}, u32[]{:S(2)}) copy-start(s32[23552]{0:T(1024)S(1)} %get-tuple-element.16510) | copy-start | bytes 282628 | tf_op jit(solution)/shard_map/cond
  291.7 49.9 %copy-start.252 = (s32[4096]{0:T(1024)}, s32[4096]{0:T(1024)S(1)}, u32[]{:S(2)}) copy-start(s32[4096]{0:T(1024)S(1)} %get-tuple-element.668.pos_ref) | copy-start | bytes 49156 | tf_op jit(solution)/shard_map/cond
  349.8 93.2 %collective-permute-start.53 = (bf16[2816,768]{1,0:T(8,128)(2,1)}, bf16[2816,768]{1,0:T(8,128)(2,1)}, u32[]{:S(2)}, u32[]{:S(2)}) collective-permute-start(bf16[2816,768]{1,0:T(8,128)(2,1)} %collective-permute-done.52.refs_3_), channel_id=1, source_target_pairs={{0,1},{1,0},{2,3},{3,2},{4,5},{5,4},{6,7},{7,6}} | collective-permute-start | bytes 12976136 | tf_op jit(solution)/shard_map/cond/branch_5_fun/ppermute | solution.py:378
  438.8 111.1 %collective-permute-start.54 = (bf16[4096,768]{1,0:T(8,128)(2,1)}, bf16[4096,768]{1,0:T(8,128)(2,1)}, u32[]{:S(2)}, u32[]{:S(2)}) collective-permute-start(bf16[4096,768]{1,0:T(8,128)(2,1)} %ffn.28.refs_0_), channel_id=1, source_target_pairs={{0,1},{1,0},{2,3},{3,2},{4,5},{5,4},{6,7},{7,6}} | collective-permute-start | bytes 18874376 | tf_op jit(solution)/shard_map/cond/branch_5_fun/ppermute | solution.py:393
  482.3 65.1 %copy-start.184 = (s32[2,4096]{1,0:T(2,128)S(1)}, s32[2,4096]{1,0:T(2,128)}, u32[]{:S(2)}) copy-start(s32[2,4096]{1,0:T(2,128)} %copy-done.183) | copy-start | bytes 98308 | tf_op jit(solution)/shard_map/cond
  482.3 65.1 %copy-start.197 = (s32[2,4096]{1,0:T(2,128)S(1)}, s32[2,4096]{1,0:T(2,128)}, u32[]{:S(2)}) copy-start(s32[2,4096]{1,0:T(2,128)} %rev.50) | copy-start | bytes 98308 | tf_op jit(solution)/shard_map/cond
  482.3 65.8 %copy-start.193 = (s32[8192]{0:T(1024)S(1)}, s32[8192]{0:T(1024)}, u32[]{:S(2)}) copy-start(s32[8192]{0:T(1024)} %get-tuple-element.16489) | copy-start | bytes 98308 | tf_op jit(solution)/shard_map/cond
  543.1 31.2 %collective-permute-start.55 = (bf16[4096,768]{1,0:T(8,128)(2,1)}, bf16[4096,768]{1,0:T(8,128)(2,1)}, u32[]{:S(2)}, u32[]{:S(2)}) collective-permute-start(bf16[4096,768]{1,0:T(8,128)(2,1)} %ffn.29.refs_1_.refs_0_), channel_id=1, source_target_pairs={{0,1},{1,0},{2,3},{3,2},{4,5},{5,4},{6,7},{7,6}} | collective-permute-start | bytes 18874376 | tf_op jit(solution)/shard_map/cond/branch_5_fun/ppermute | solution.py:393
  549.7 19.6 %copy-start.47 = (s32[8192]{0:T(1024)S(1)}, s32[8192]{0:T(1024)}, u32[]{:S(2)}) copy-start(s32[8192]{0:T(1024)} %copy-done.46) | copy-start | bytes 98308 | tf_op jit(solution)/shard_map/cond
  549.7 19.6 %copy-start.65 = (s32[8192]{0:T(1024)S(1)}, s32[8192]{0:T(1024)}, u32[]{:S(2)}) copy-start(s32[8192]{0:T(1024)} %copy-done.64) | copy-start | bytes 98308 | tf_op jit(solution)/shard_map/cond
  549.7 19.6 %copy-start.77 = (s32[8192]{0:T(1024)S(1)}, s32[8192]{0:T(1024)}, u32[]{:S(2)}) copy-start(s32[8192]{0:T(1024)} %get-tuple-element.1500) | copy-start | bytes 98308 | tf_op jit(solution)/shard_map/cond
  549.7 19.6 %copy-start.86 = (s32[8192]{0:T(1024)S(1)}, s32[8192]{0:T(1024)}, u32[]{:S(2)}) copy-start(s32[8192]{0:T(1024)} %get-tuple-element.960) | copy-start | bytes 98308 | tf_op jit(solution)/shard_map/cond
  549.8 19.6 %copy-start.95 = (s32[8192]{0:T(1024)S(1)}, s32[8192]{0:T(1024)}, u32[]{:S(2)}) copy-start(s32[8192]{0:T(1024)} %get-tuple-element.1023) | copy-start | bytes 98308 | tf_op jit(solution)/shard_map/cond
  549.8 19.6 %copy-start.104 = (s32[8192]{0:T(1024)S(1)}, s32[8192]{0:T(1024)}, u32[]{:S(2)}) copy-start(s32[8192]{0:T(1024)} %get-tuple-element.1572) | copy-start | bytes 98308 | tf_op jit(solution)/shard_map/cond
  567.7 113.1 %collective-permute-start.56 = (bf16[3328,768]{1,0:T(8,128)(2,1)}, bf16[3328,768]{1,0:T(8,128)(2,1)}, u32[]{:S(2)}, u32[]{:S(2)}) collective-permute-start(bf16[3328,768]{1,0:T(8,128)(2,1)} %compact.58), channel_id=1, source_target_pairs={{0,2},{1,3},{2,0},{3,1},{4,6},{5,7},{6,4},{7,5}} | collective-permute-start | bytes 15335432 | tf_op jit(solution)/shard_map/cond/branch_5_fun/ppermute | solution.py:395
  574.3 106.5 %copy-start.143 = (s32[64,128]{1,0:T(8,128)S(1)}, s32[64,128]{1,0:T(8,128)}, u32[]{:S(2)}) copy-start(s32[64,128]{1,0:T(8,128)} %get-tuple-element.644) | copy-start | bytes 98308 | tf_op jit(solution)/shard_map/cond
  592.4 197.0 %collective-permute-start.58 = (bf16[3328,768]{1,0:T(8,128)(2,1)}, bf16[3328,768]{1,0:T(8,128)(2,1)}, u32[]{:S(2)}, u32[]{:S(2)}) collective-permute-start(bf16[3328,768]{1,0:T(8,128)(2,1)} %compact.59), channel_id=1, source_target_pairs={{0,2},{1,3},{2,0},{3,1},{4,6},{5,7},{6,4},{7,5}} | collective-permute-start | bytes 15335432 | tf_op jit(solution)/shard_map/cond/branch_5_fun/ppermute | solution.py:395
  680.8 108.6 %collective-permute-start.57 = (bf16[3328,768]{1,0:T(8,128)(2,1)}, bf16[3328,768]{1,0:T(8,128)(2,1)}, u32[]{:S(2)}, u32[]{:S(2)}) collective-permute-start(bf16[3328,768]{1,0:T(8,128)(2,1)} %collective-permute-done.56.refs_4_), channel_id=1, source_target_pairs={{0,1},{1,0},{2,3},{3,2},{4,5},{5,4},{6,7},{7,6}} | collective-permute-start | bytes 15335432 | tf_op jit(solution)/shard_map/cond/branch_5_fun/ppermute | solution.py:396
  789.4 106.8 %collective-permute-start.59 = (bf16[3328,768]{1,0:T(8,128)(2,1)}, bf16[3328,768]{1,0:T(8,128)(2,1)}, u32[]{:S(2)}, u32[]{:S(2)}) collective-permute-start(bf16[3328,768]{1,0:T(8,128)(2,1)} %collective-permute-done.58.refs_0_), channel_id=1, source_target_pairs={{0,1},{1,0},{2,3},{3,2},{4,5},{5,4},{6,7},{7,6}} | collective-permute-start | bytes 15335432 | tf_op jit(solution)/shard_map/cond/branch_5_fun/ppermute | solution.py:396
  (14 other events, 191.6 us)

commit v3 on v2

--- a/solution.py
+++ b/solution.py
@@ -7,8 +7,9 @@
 from jax.experimental.pallas import tpu as pltpu
 from jax.sharding import PartitionSpec as P
 
+
 LANES = 128
-ROW = 8
+ROW = 6
 BLOCK = 512
 WINDOW = BLOCK // 2 + 16
 FAR = 1 << 20
@@ -53,8 +54,8 @@
     return jnp.where(low, th * LANES + tl, 0).sum(1).astype(jnp.int32)
 
 
-def params(**kw):
-    return pltpu.CompilerParams(dimension_semantics=("arbitrary",), vmem_limit_bytes=VMEM, **kw)
+def call(kernel, *args, **kw):
+    return pl.pallas_call(kernel, compiler_params=pltpu.CompilerParams(dimension_semantics=("arbitrary",), vmem_limit_bytes=VMEM), **kw)(*args)
 
 
 def cost(flops, size):
@@ -83,13 +84,12 @@
 
 
 def line(r):
-    return pl.ds(pl.multiple_of(r * ROW, ROW), ROW)
+    return pl.ds(r * ROW, ROW)
 
 
 def compact_kernel(first, last, base_ref, pos_ref, *refs):
     parts, out_ref, acc = refs[:-2], refs[-2], refs[-1]
     i = pl.program_id(0)
-    d = out_ref.shape[1]
 
     @pl.when(i == 0)
     def _():
@@ -120,8 +120,8 @@
     def spec(k):
         return pl.BlockSpec((BLOCK, d), lambda i, *_: (jnp.clip(i - first[k], 0, counts[k] - 1), 0))
 
-    return pl.pallas_call(
-        functools.partial(compact_kernel, first, first[-1] - 1),
+    return call(
+        functools.partial(compact_kernel, first, first[-1] - 1), base, pos[:, None, :], *parts,
         grid_spec=pltpu.PrefetchScalarGridSpec(
             num_scalar_prefetch=1,
             grid=(first[-1],),
@@ -130,10 +130,8 @@
             scratch_shapes=[pltpu.VMEM((rows + WINDOW, d), jnp.float32)],
         ),
         out_shape=jax.ShapeDtypeStruct((rows, d), parts[0].dtype),
-        compiler_params=params(),
         cost_estimate=cost(2e10, 2 * d * (sum(p.shape[0] for p in parts) + rows)),
-        name="compact",
-    )(base, pos[:, None, :], *parts)
+    )
 
 
 def gather_kernel(first, stride, has_init, pos_ref, slot_ref, start_ref, *refs):
@@ -143,6 +141,7 @@
         @pl.when(i < first[1])
         def _():
             split_rows(refs[0], acc, i * BLOCK * ROW)
+
         refs, first = refs[1:], first[1:]
     else:
         @pl.when(i == 0)
@@ -177,7 +176,7 @@
         join_rows(acc, (i - first[len(refs)]) * BLOCK * ROW, out_ref)
 
 
-def gather(init, part_rows, parts, key, slots, stride):
+def gather(init, parts, key, slots, stride):
     d = parts[0].shape[1]
     counts = [blocks_of(p.shape[0]) for p in parts]
     has_init = init is not None
@@ -194,8 +193,8 @@
         return pl.BlockSpec((BLOCK, d), lambda i, *_: (jnp.clip(i - first[k], 0, counts[k] - 1) + off, 0))
 
     offs = [init[1] if has_init else 0] + [0] * len(parts)
-    return pl.pallas_call(
-        functools.partial(gather_kernel, first, stride, has_init),
+    return call(
+        functools.partial(gather_kernel, first, stride, has_init), key, slot, starts, *ins,
         grid_spec=pltpu.PrefetchScalarGridSpec(
             num_scalar_prefetch=3,
             grid=(first[-1],),
@@ -204,10 +203,8 @@
             scratch_shapes=[pltpu.VMEM((slots * ROW, LANES), jnp.float32), pltpu.VMEM((BLOCK * ROW, LANES), jnp.float32)],
         ),
         out_shape=jax.ShapeDtypeStruct((slots, d), parts[0].dtype),
-        compiler_params=params(),
         cost_estimate=cost(4e10, 2 * d * (sum(p.shape[0] for p in ins) + slots)),
-        name="gather",
-    )(key, slot, starts, *ins)
+    )
 
 
 def ffn_kernel(x_ref, w_in_ref, w_out_ref, gate_ref, out_ref):
@@ -225,8 +222,8 @@
 def ffn(x, w_in, w_out, gate, turn, turns):
     count, cap = gate.shape[0], gate.shape[1]
     d, f = w_in.shape[1], w_in.shape[2]
-    return pl.pallas_call(
-        ffn_kernel,
+    return call(
+        ffn_kernel, x, w_in, w_out, gate,
         grid=(count,),
         in_specs=[
             pl.BlockSpec((cap, d), lambda i: (i, 0)),
@@ -236,10 +233,8 @@
         ],
         out_specs=pl.BlockSpec((cap, d), lambda i: (i, 0)),
         out_shape=jax.ShapeDtypeStruct((count * cap, d), x.dtype),
-        compiler_params=params(),
         cost_estimate=cost(4 * count * cap * d * f, 4 * count * d * f),
-        name="ffn",
-    )(x, w_in, w_out, gate)
+    )
 
 
 def combine_kernel(first, dest_ref, dup_ref, tok_ref, *refs):
@@ -265,6 +260,7 @@
                     for u in range(8):
                         acc[where[u], :] = sums[u]
                     return c
+
                 lax.fori_loop(0, BLOCK // 8, body, 0)
 
             @pl.when(dup_ref[step] != 0)
@@ -273,6 +269,7 @@
                     w = line(dest_ref[start + r])
                     acc[w, :] = acc[w, :] + rows[line(r), :]
                     return c
+
                 lax.fori_loop(0, BLOCK, body, 0)
 
     @pl.when(i >= first[-2])
@@ -294,8 +291,8 @@
     def spec(k):
         return pl.BlockSpec((BLOCK, d), lambda i, *_: (jnp.clip(i - first[k], 0, counts[k] - 1), 0))
 
-    return pl.pallas_call(
-        functools.partial(combine_kernel, first),
+    return call(
+        functools.partial(combine_kernel, first), dest, dup, init, *parts,
         grid_spec=pltpu.PrefetchScalarGridSpec(
             num_scalar_prefetch=2,
             grid=(first[-1],),
@@ -304,10 +301,16 @@
             scratch_shapes=[pltpu.VMEM(((n + 1) * ROW, LANES), jnp.float32), pltpu.VMEM((BLOCK * ROW, LANES), jnp.float32)],
         ),
         out_shape=jax.ShapeDtypeStruct((n, d), dtype),
-        compiler_params=params(),
         cost_estimate=cost(1e11, 2 * d * dest.shape[0]),
-        name="combine",
-    )(dest, dup, init, *parts)
+    )
+
+
+def share(x, axis, count):
+    return lax.all_to_all(jnp.broadcast_to(x[None], (count,) + x.shape), axis, 0, 0)
+
+
+def hop(x, pairs):
+    return lax.ppermute(x, "ep", pairs)
 
 
 def solution(mesh):
@@ -318,7 +321,7 @@
     swap_chip = [(g, g ^ 2) for g in range(group_n)]
 
     def local_layer(tok_loc, sel_loc, gate_loc, win_loc, wout_loc):
-        n, d = tok_loc.shape
+        n, _ = tok_loc.shape
         exp_count, cap_slots = sel_loc.shape
         turns = 2
         experts = exp_count // turns
@@ -334,7 +337,7 @@
 
         sib_tok = lax.ppermute(tok_loc, "ep", swap_core)
         mine = by_turn(sel_loc)
-        all_sel = lax.all_gather(mine, "ep").reshape(2, 2, turns, part)
+        all_sel = share(mine, "ep", group_n).reshape(2, 2, turns, part)
         chip_sel = lax.dynamic_index_in_dim(all_sel, chip, 0, keepdims=False)
         far_sel = lax.dynamic_index_in_dim(all_sel, 1 - chip, 0, keepdims=False)
         sib = lax.dynamic_index_in_dim(chip_sel, 1 - core, 0, keepdims=False)
@@ -359,7 +362,7 @@
                           jnp.maximum(jnp.maximum(back_n[0], come_n[0]), jnp.maximum(back_n[1], come_n[1]))])
         caps = 2 * jnp.array(levels, jnp.int32)
         level = (caps[:-1] < most[None, :]).any(1).sum().astype(jnp.int32)
-        level = lax.pmax(level, ("dp", "ep"))
+        level = share(jnp.full((1, LANES), level), ("dp", "ep"), mesh.size).max()
 
         def my_turn(flags, rank):
             flags, rank = flags.reshape(-1), rank.reshape(-1)
@@ -374,13 +377,13 @@
         def run_level(rows):
             def run(tok, sib_tok, give_pos, want, want_rank, mine, sib, far_sel, back_far, back_rank, come_far, come_rank, come_n, gate, w_in, w_out):
                 sent = [compact([tok, sib_tok], give_pos[h], rows[h]) for h in range(turns)]
-                got = [lax.ppermute(x, "ep", swap_chip) for x in sent]
-                sib_got = [lax.ppermute(x, "ep", swap_core) for x in got]
+                got = [hop(x, swap_chip) for x in sent]
+                sib_got = [hop(x, swap_core) for x in got]
 
                 near_key = jnp.where(mine // chip_n == chip, (mine - me * n) % chip_n, FAR).reshape(-1)
-                x_near = gather(None, n, [tok, sib_tok], near_key, turns * part, n // BLOCK)
+                x_near = gather(None, [tok, sib_tok], near_key, turns * part, n // BLOCK)
                 code = jnp.where(want[0], want_rank[0], want_rank[1] + 2 * part)
-                lists, x, p = [], [], []
+                x, p = [], []
                 for h in range(turns):
                     is_far = mine[h] // chip_n != chip
                     c = lookup(code, mine[h] - (1 - chip) * chip_n)
@@ -388,12 +391,12 @@
                     key = (late * 2 + jnp.where(rank % 2 == core, 0, 1)) * part + rank // 2
                     key = jnp.where(is_far, key, FAR)
                     tables = [t for k in range(h + 1) for t in (got[k], sib_got[k])]
-                    x.append(gather((x_near, h * (part // BLOCK)), part, tables, key, part, part // BLOCK))
+                    x.append(gather((x_near, h * (part // BLOCK)), tables, key, part, part // BLOCK))
                     p.append(ffn(x[h], w_in, w_out, gate[h], h, turns))
-                sib_p = [lax.ppermute(y, "ep", swap_core) for y in p]
+                sib_p = [hop(y, swap_core) for y in p]
                 back = [compact([p[h], sib_p[h]], my_turn(back_far[h], back_rank[h]), rows[2]) for h in range(turns)]
-                back_got = [lax.ppermute(y, "ep", swap_chip) for y in back]
-                sib_back = [lax.ppermute(y, "ep", swap_core) for y in back_got]
+                back_got = [hop(y, swap_chip) for y in back]
+                sib_back = [hop(y, swap_core) for y in back_got]
                 ids = jnp.arange(2 * part, dtype=jnp.int32)
                 come = []
                 for h in range(turns):
@@ -406,10 +409,12 @@
                 acc = combine(tok, [p[0], p[1], sib_p[0], sib_p[1], back_got[0], sib_back[0]],
                               [own_to[0], own_to[1], sib_to[0], sib_to[1]] + come[0], jnp.float32)
                 return combine(acc, [back_got[1], sib_back[1]], come[1], tok.dtype)
+
             return run
 
         gate = jnp.swapaxes(gate_loc.reshape(experts, turns, cap_slots), 0, 1)[..., None]
-        return lax.switch(level, [run_level(r) for r in levels], tok_loc, sib_tok, give_pos, want, want_rank, mine, sib, far_sel,
+        branches = [run_level(r) for r in levels]
+        return lax.switch(level, branches, tok_loc, sib_tok, give_pos, want, want_rank, mine, sib, far_sel,
                           back_far, back_rank, come_far, come_rank, come_n, gate, win_loc, wout_loc)
 
     return jax.shard_map(local_layer, mesh=mesh, in_specs=(row_spec, row_spec, row_spec, expert_spec, expert_spec), out_specs=row_spec, check_vma=False)

time: 941 us -> 778 us (0.83)
  the two profiles are of different devices: /device:TPU:0 before, /device:TPU:5 now
where the time goes in v3:
time: 778 us; the launch traced here: 766 us
  Pallas kernels  423 us (54%)
  waiting for transfers between devices  170 us (22%)
  other arithmetic  43 us (6%)
  local copies, waits for them, and re-layouts  35.9 us (5%)
  matrix products  35.6 us (5%)
  loops' own time  33.2 us (4%)
  starting transfers between devices  17.1 us (2%)
    pallas_call x11, Pallas kernels, call(): pl.pallas_call(kernel, compiler_params=pltpu.CompilerParams(dimension_sem...  423 us
    ppermute x10, waiting for transfers between devices, hop(): return lax.ppermute(x, 'ep', pairs)  157 us
    dot_general x28, matrix products, bdot(): jnp.einsum(spec, a.astype(jnp.bfloat16), b.astype(jnp.bfloat16), preferre...  35.6 us
    another operation x1, loops' own time, local_layer(): lax.switch(level, branches, tok_loc, sib_tok, give_pos, want, want_rank,...  33.2 us
    sort x3, other arithmetic, gather(): key, slot = lax.sort((key, jnp.arange(slots, dtype=jnp.int32)), num_keys=1)  18.3 us
  transfers between devices with their start and end apart: 13, of which 5 were waited for; matrix products, arithmetic and copies ran while one was open for 15% of the time, Pallas kernels for 47%

profile of v3, /device:TPU:5, one launch (start us, length us, event | category | flops | bytes accessed | tf_op | source)
XLA Modules:
  0.0 765.7 jit_solution(13019514863778666345)
XLA Ops:
  2.2 3.3 all-to-all-start
  6.3 13.5 %all-to-all-done = s32[4,2,4096]{2,1,0:T(2,128)S(1)} async-done(((s32[4,2,4096]{2,1,0:T(2,128)}), s32[4,2,4096]{2,1,0:T(2,128)S(1)}, u32[]{:S(2)}, u32[]{:S(2)}) %all-to-all-start) | async-done | bytes 131104 | tf_op jit(solution)/shard_map/all_to_all | solution.py:309
  24.7 4.1 convert_reduce_fusion.31
  28.9 4.1 convert_reduce_fusion.27
  33.9 4.1 convert_reduce_fusion.29
  38.0 4.1 fusion.1694
  46.3 3.1 all-to-all-start.1
  59.9 704.4 %conditional.1 = (bf16[8192,768]{1,0:T(8,128)(2,1)}) conditional(s32[]{:T(128)} %clamp.173, (s32[]{:T(128)}, s32[64,128]{1,0:T(8,128)}, s32[8192]{0:T(1024)}, s32[2,2,4096]{2,1,0:T(2,128)}, s32[]{:T(128)}, /*index=5*/s32[]{:T(128)}, s32[2,4096]{1,0:T(2,128)S(1)}, s32[]{:T(128)}, s32[2,2,2,4096]{3,2,1,0:T(2,128)}, ...), branch_computations={%region_19.46_spmd, %region_46.73_spmd, %region_73.100_spmd, %regi... | conditional | flops 478412570624 | bytes 837832320 | solution.py:417
  70.6 29.9 %branch_2_fun.12 = bf16[2432,768]{1,0:T(8,128)(2,1)} custom-call(s32[32]{0:T(128)} %get-tuple-element.17100.base_ref, s32[32,1,512]{2,1,0:T(1,128)} %reshape_reshape.81.pos_ref, bf16[8192,768]{1,0:T(8,128)(2,1)} %get-tuple-element.559.refs_0_.tok_ref, bf16[8192,768]{1,0:T(8,128)(2,1)} %get-tuple-element.567.refs_1_), custom_call_target="tpu_custom_call" | custom-call | flops 20000000000 | bytes 28901376 | tf_op jit(solution)/shard_map/cond/branch_2_fun/pallas_call | solution.py:58
  102.4 29.7 %branch_2_fun.15 = bf16[2176,768]{1,0:T(8,128)(2,1)} custom-call(s32[32]{0:T(128)} %get-tuple-element.17099.base_ref, s32[32,1,512]{2,1,0:T(1,128)} %reshape_reshape.83.pos_ref, bf16[8192,768]{1,0:T(8,128)(2,1)} %get-tuple-element.559.refs_0_.tok_ref, bf16[8192,768]{1,0:T(8,128)(2,1)} %get-tuple-element.567.refs_1_), custom_call_target="tpu_custom_call" | custom-call | flops 20000000000 | bytes 28508160 | tf_op jit(solution)/shard_map/cond/branch_2_fun/pallas_call | solution.py:58
  138.3 9.4 %rev.45 = s32[2,4096]{1,0:T(2,128)} reverse(s32[2,4096]{1,0:T(2,128)S(1)} %reshape.3672), dimensions={0} | reverse | bytes 65536 | tf_op jit(solution)/shard_map/cond/branch_2_fun/rev | solution.py:370
  150.9 5.8 sort.384
  156.6 6.8 sort.385
  166.8 5.8 sort.386
  175.5 7.2 collective-permute-done.20.refs_1_
  184.9 34.1 %branch_2_fun.11.refs_0_ = bf16[8192,768]{1,0:T(8,128)(2,1)} custom-call(s32[8192]{0:T(1024)} %copy-done.229, s32[8192]{0:T(1024)} %get-tuple-element.566.slot_ref, s32[33]{0:T(128)} %convert_reduce_fusion.6.start_ref, bf16[8192,768]{1,0:T(8,128)(2,1)} %get-tuple-element.559.refs_0_.tok_ref, bf16[8192,768]{1,0:T(8,128)(2,1)} %get-tuple-element.567.refs_1_), custom_call_target="tpu_custom_call" | custom-call | flops 40000000000 | bytes 37748736 | tf_op jit(solution)/shard_map/cond/branch_2_fun/pallas_call | solution.py:58
  219.0 35.4 %collective-permute-done.22.refs_3_ = bf16[2176,768]{1,0:T(8,128)(2,1)} collective-permute-done((bf16[2176,768]{1,0:T(8,128)(2,1)}, bf16[2176,768]{1,0:T(8,128)(2,1)}, u32[]{:S(2)}, u32[]{:S(2)}) %collective-permute-start.22) | collective-permute-done | bytes 3342368 | tf_op jit(solution)/shard_map/cond/branch_2_fun/ppermute | solution.py:313
  255.6 24.8 %branch_2_fun.13.x_ref = bf16[4096,768]{1,0:T(8,128)(2,1)} custom-call(s32[4096]{0:T(1024)} %copy-done.240, s32[4096]{0:T(1024)} %get-tuple-element.564.slot_ref, s32[17]{0:T(128)} %convert_reduce_fusion.8.start_ref, bf16[8192,768]{1,0:T(8,128)(2,1)} %branch_2_fun.11.refs_0_, bf16[2432,768]{1,0:T(8,128)(2,1)} %collective-permute-done.20.refs_1_, ...), custom_call_target="tpu_custom_call" | custom-call | flops 40000000000 | bytes 26345472 | tf_op jit(solution)/shard_map/cond/branch_2_fun/pallas_call | solution.py:58
  280.5 60.5 %branch_2_fun.14.refs_0_ = bf16[4096,768]{1,0:T(8,128)(2,1)} custom-call(bf16[4096,768]{1,0:T(8,128)(2,1)} %branch_2_fun.13.x_ref, bf16[32,768,3072]{2,1,0:T(8,128)(2,1)} %get-tuple-element.1026.w_in_ref, bf16[32,3072,768]{2,1,0:T(8,128)(2,1)} %get-tuple-element.1035.w_out_ref, f32[16,256,1]{2,1,0:T(8,128)} %copy.1421.gate_ref), custom_call_target="tpu_custom_call" | custom-call | flops 38654705664 | bytes 150994944 | tf_op jit(solution)/shard_map/cond/branch_2_fun/pallas_call | solution.py:58
  341.0 32.6 %branch_2_fun.16.x_ref = bf16[4096,768]{1,0:T(8,128)(2,1)} custom-call(s32[4096]{0:T(1024)} %copy-done.244, s32[4096]{0:T(1024)} %get-tuple-element.573.slot_ref, s32[33]{0:T(128)} %convert_reduce_fusion.7.start_ref, bf16[8192,768]{1,0:T(8,128)(2,1)} %branch_2_fun.11.refs_0_, bf16[2432,768]{1,0:T(8,128)(2,1)} %collective-permute-done.20.refs_1_, ...), custom_call_target="tpu_custom_call" | custom-call | flops 40000000000 | bytes 33030144 | tf_op jit(solution)/shard_map/cond/branch_2_fun/pallas_call | solution.py:58
  373.6 60.5 %branch_2_fun.17.refs_1_.refs_0_ = bf16[4096,768]{1,0:T(8,128)(2,1)} custom-call(bf16[4096,768]{1,0:T(8,128)(2,1)} %branch_2_fun.16.x_ref, bf16[32,768,3072]{2,1,0:T(8,128)(2,1)} %get-tuple-element.1026.w_in_ref, bf16[32,3072,768]{2,1,0:T(8,128)(2,1)} %get-tuple-element.1035.w_out_ref, f32[16,256,1]{2,1,0:T(8,128)} %copy.1422.gate_ref), custom_call_target="tpu_custom_call" | custom-call | flops 38654705664 | bytes 150994944 | tf_op jit(solution)/shard_map/cond/branch_2_fun/pallas_call | solution.py:58
  435.0 17.3 %branch_2_fun.18 = bf16[2560,768]{1,0:T(8,128)(2,1)} custom-call(s32[16]{0:T(128)} %compare_select_fusion.54.base_ref, s32[16,1,512]{2,1,0:T(1,128)} %reshape.3670.pos_ref, bf16[4096,768]{1,0:T(8,128)(2,1)} %branch_2_fun.14.refs_0_, bf16[4096,768]{1,0:T(8,128)(2,1)} %collective-permute-done.24.refs_1_.refs_2_), custom_call_target="tpu_custom_call" | custom-call | flops 20000000000 | bytes 16515072 | tf_op jit(solution)/shard_map/cond/branch_2_fun/pallas_call | solution.py:58
  455.6 2.4 fusion.414
  458.0 3.5 sub.1540
  464.0 2.4 fusion.426
  466.4 3.4 sub.1526
  470.4 17.3 %branch_2_fun.20 = bf16[2560,768]{1,0:T(8,128)(2,1)} custom-call(s32[16]{0:T(128)} %compare_select_fusion.53.base_ref, s32[16,1,512]{2,1,0:T(1,128)} %reshape.3674.pos_ref, bf16[4096,768]{1,0:T(8,128)(2,1)} %branch_2_fun.17.refs_1_.refs_0_, bf16[4096,768]{1,0:T(8,128)(2,1)} %collective-permute-done.25.refs_3_.refs_1_), custom_call_target="tpu_custom_call" | custom-call | flops 20000000000 | bytes 16515072 | tf_op jit(solution)/shard_map/cond/branch_2_fun/pallas_call | solution.py:58
  489.1 49.5 %collective-permute-done.26.refs_4_ = bf16[2560,768]{1,0:T(8,128)(2,1)} collective-permute-done((bf16[2560,768]{1,0:T(8,128)(2,1)}, bf16[2560,768]{1,0:T(8,128)(2,1)}, u32[]{:S(2)}, u32[]{:S(2)}) %collective-permute-start.26) | collective-permute-done | bytes 3932192 | tf_op jit(solution)/shard_map/cond/branch_2_fun/ppermute | solution.py:313
  541.0 3.2 and_select_fusion.16
  558.5 64.5 %collective-permute-done.28.refs_0_ = bf16[2560,768]{1,0:T(8,128)(2,1)} collective-permute-done((bf16[2560,768]{1,0:T(8,128)(2,1)}, bf16[2560,768]{1,0:T(8,128)(2,1)}, u32[]{:S(2)}, u32[]{:S(2)}) %collective-permute-start.28) | collective-permute-done | bytes 3932192 | tf_op jit(solution)/shard_map/cond/branch_2_fun/ppermute | solution.py:313
  624.3 80.5 %branch_2_fun.19.tok_ref = f32[8192,768]{1,0:T(8,128)} custom-call(s32[21504]{0:T(1024)} %copy-done.221, s32[42]{0:T(128)} %convert_element_type.408.dup_ref, bf16[8192,768]{1,0:T(8,128)(2,1)} %get-tuple-element.559.refs_0_.tok_ref, bf16[4096,768]{1,0:T(8,128)(2,1)} %branch_2_fun.14.refs_0_, bf16[4096,768]{1,0:T(8,128)(2,1)} %branch_2_fun.17.refs_1_.refs_0_, ...), custom_call_target="tpu_custom_call" | custom-call | flops 99999997952 | bytes 33030144 | tf_op jit(solution)/shard_map/cond/branch_2_fun/pallas_call | solution.py:58
  704.9 35.9 %branch_2_fun.21 = bf16[8192,768]{1,0:T(8,128)(2,1)} custom-call(s32[5120]{0:T(1024)} %pad_add_fusion.4.dest_ref, s32[10]{0:T(128)} %convert_element_type.404.dup_ref, f32[8192,768]{1,0:T(8,128)} %branch_2_fun.19.tok_ref, bf16[2560,768]{1,0:T(8,128)(2,1)} %collective-permute-done.28.refs_0_, bf16[2560,768]{1,0:T(8,128)(2,1)} %collective-permute-done.29.refs_1_), custom_call_target="tpu_custom_call" | custom-call | flops 99999997952 | bytes 7864320 | tf_op jit(solution)/shard_map/cond/branch_2_fun/pallas_call | solution.py:58
  (230 shorter events, 66.0 us)
Async XLA Ops:
  0.0 59.8 %collective-permute-start.90 = (bf16[8192,768]{1,0:T(8,128)(2,1)}, bf16[8192,768]{1,0:T(8,128)(2,1)}, u32[]{:S(2)}, u32[]{:S(2)}) collective-permute-start(bf16[8192,768]{1,0:T(8,128)(2,1)} %param.15), channel_id=1, source_target_pairs={{0,1},{1,0},{2,3},{3,2},{4,5},{5,4},{6,7},{7,6}} | collective-permute-start | bytes 37748744 | tf_op jit(solution)/shard_map/ppermute | solution.py:338
  2.2 17.6 %all-to-all-start = ((s32[4,2,4096]{2,1,0:T(2,128)}), s32[4,2,4096]{2,1,0:T(2,128)S(1)}, u32[]{:S(2)}, u32[]{:S(2)}) async-start(s32[4,2,4096]{2,1,0:T(2,128)} %broadcast_in_dim.922), calls=%async_computation | async-start | bytes 262144 | tf_op jit(solution)/shard_map/all_to_all | solution.py:309
  24.0 29.1 %copy-start.128 = (s32[2,1,4096]{2,1,0:T(1,128)}, s32[2,1,4096]{2,1,0:T(1,128)S(1)}, u32[]{:S(2)}) copy-start(s32[2,1,4096]{2,1,0:T(1,128)S(1)} %get-tuple-element.17328) | copy-start | bytes 98308
  24.0 29.7 %copy-start.118 = (s32[2,1,4096]{2,1,0:T(1,128)}, s32[2,1,4096]{2,1,0:T(1,128)S(1)}, u32[]{:S(2)}) copy-start(s32[2,1,4096]{2,1,0:T(1,128)S(1)} %get-tuple-element.17327) | copy-start | bytes 98308
  46.3 12.2 %all-to-all-start.1 = ((s32[8,1,128]{2,1,0:T(1,128)}), s32[8,1,128]{2,1,0:T(1,128)S(1)}, u32[]{:S(2)}, u32[]{:S(2)}) async-start(s32[8,1,128]{2,1,0:T(1,128)} %broadcast_in_dim_broadcast_in_dim_broadcast_in_dim.3), calls=%async_computation.1 | async-start | bytes 8192 | tf_op jit(solution)/shard_map/all_to_all | solution.py:309
  68.8 63.6 %copy-start.4 = (s32[8192]{0:T(1024)}, s32[8192]{0:T(1024)S(1)}, u32[]{:S(2)}) copy-start(s32[8192]{0:T(1024)S(1)} %get-tuple-element.17381) | copy-start | bytes 98308 | tf_op jit(solution)/shard_map/cond
  68.8 63.6 %copy-start.22 = (s32[8192]{0:T(1024)}, s32[8192]{0:T(1024)S(1)}, u32[]{:S(2)}) copy-start(s32[8192]{0:T(1024)S(1)} %get-tuple-element.17390) | copy-start | bytes 98308 | tf_op jit(solution)/shard_map/cond
  68.8 63.6 %copy-start.40 = (s32[8192]{0:T(1024)}, s32[8192]{0:T(1024)S(1)}, u32[]{:S(2)}) copy-start(s32[8192]{0:T(1024)S(1)} %get-tuple-element.17399) | copy-start | bytes 98308 | tf_op jit(solution)/shard_map/cond
  68.8 63.6 %copy-start.58 = (s32[8192]{0:T(1024)}, s32[8192]{0:T(1024)S(1)}, u32[]{:S(2)}) copy-start(s32[8192]{0:T(1024)S(1)} %get-tuple-element.17408) | copy-start | bytes 98308 | tf_op jit(solution)/shard_map/cond
  100.5 82.2 %collective-permute-start.20 = (bf16[2432,768]{1,0:T(8,128)(2,1)}, bf16[2432,768]{1,0:T(8,128)(2,1)}, u32[]{:S(2)}, u32[]{:S(2)}) collective-permute-start(bf16[2432,768]{1,0:T(8,128)(2,1)} %branch_2_fun.12), channel_id=1, source_target_pairs={{0,2},{1,3},{2,0},{3,1},{4,6},{5,7},{6,4},{7,5}} | collective-permute-start | bytes 11206664 | tf_op jit(solution)/shard_map/cond/branch_2_fun/ppermute | solution.py:313
  132.1 122.3 %collective-permute-start.22 = (bf16[2176,768]{1,0:T(8,128)(2,1)}, bf16[2176,768]{1,0:T(8,128)(2,1)}, u32[]{:S(2)}, u32[]{:S(2)}) collective-permute-start(bf16[2176,768]{1,0:T(8,128)(2,1)} %branch_2_fun.15), channel_id=1, source_target_pairs={{0,2},{1,3},{2,0},{3,1},{4,6},{5,7},{6,4},{7,5}} | collective-permute-start | bytes 10027016 | tf_op jit(solution)/shard_map/cond/branch_2_fun/ppermute | solution.py:313
  166.7 52.2 %copy-start.219 = (s32[21504]{0:T(1024)}, s32[21504]{0:T(1024)S(1)}, u32[]{:S(2)}) copy-start(s32[21504]{0:T(1024)S(1)} %get-tuple-element.17090) | copy-start | bytes 258052 | tf_op jit(solution)/shard_map/cond
  172.5 46.4 %copy-start.244 = (s32[4096]{0:T(1024)}, s32[4096]{0:T(1024)S(1)}, u32[]{:S(2)}) copy-start(s32[4096]{0:T(1024)S(1)} %get-tuple-element.572.pos_ref) | copy-start | bytes 49156 | tf_op jit(solution)/shard_map/cond
  182.8 72.9 %collective-permute-start.21 = (bf16[2432,768]{1,0:T(8,128)(2,1)}, bf16[2432,768]{1,0:T(8,128)(2,1)}, u32[]{:S(2)}, u32[]{:S(2)}) collective-permute-start(bf16[2432,768]{1,0:T(8,128)(2,1)} %collective-permute-done.20.refs_1_), channel_id=1, source_target_pairs={{0,1},{1,0},{2,3},{3,2},{4,5},{5,4},{6,7},{7,6}} | collective-permute-start | bytes 11206664 | tf_op jit(solution)/shard_map/cond/branch_2_fun/ppermute | solution.py:313
  254.4 86.6 %collective-permute-start.23 = (bf16[2176,768]{1,0:T(8,128)(2,1)}, bf16[2176,768]{1,0:T(8,128)(2,1)}, u32[]{:S(2)}, u32[]{:S(2)}) collective-permute-start(bf16[2176,768]{1,0:T(8,128)(2,1)} %collective-permute-done.22.refs_3_), channel_id=1, source_target_pairs={{0,1},{1,0},{2,3},{3,2},{4,5},{5,4},{6,7},{7,6}} | collective-permute-start | bytes 10027016 | tf_op jit(solution)/shard_map/cond/branch_2_fun/ppermute | solution.py:313
  341.0 94.0 %collective-permute-start.24 = (bf16[4096,768]{1,0:T(8,128)(2,1)}, bf16[4096,768]{1,0:T(8,128)(2,1)}, u32[]{:S(2)}, u32[]{:S(2)}) collective-permute-start(bf16[4096,768]{1,0:T(8,128)(2,1)} %branch_2_fun.14.refs_0_), channel_id=1, source_target_pairs={{0,1},{1,0},{2,3},{3,2},{4,5},{5,4},{6,7},{7,6}} | collective-permute-start | bytes 18874376 | tf_op jit(solution)/shard_map/cond/branch_2_fun/ppermute | solution.py:313
  373.6 60.6 %copy-start.260 = (s32[16]{0:T(128)S(1)}, s32[16]{0:T(128)}, u32[]{:S(2)}) copy-start(s32[16]{0:T(128)} %fusion.455) | copy-start | bytes 196 | tf_op jit(solution)/shard_map/cond
  373.6 61.1 %copy-start.111 = (s32[2,2,4096]{2,1,0:T(2,128)S(1)}, s32[2,2,4096]{2,1,0:T(2,128)}, u32[]{:S(2)}) copy-start(s32[2,2,4096]{2,1,0:T(2,128)} %get-tuple-element.550) | copy-start | bytes 196612 | tf_op jit(solution)/shard_map/cond
  373.6 61.2 %copy-start.176 = (s32[2,4096]{1,0:T(2,128)S(1)}, s32[2,4096]{1,0:T(2,128)}, u32[]{:S(2)}) copy-start(s32[2,4096]{1,0:T(2,128)} %copy-done.175) | copy-start | bytes 98308 | tf_op jit(solution)/shard_map/cond
  373.6 61.2 %copy-start.191 = (s32[2,4096]{1,0:T(2,128)S(1)}, s32[2,4096]{1,0:T(2,128)}, u32[]{:S(2)}) copy-start(s32[2,4096]{1,0:T(2,128)} %rev.45) | copy-start | bytes 98308 | tf_op jit(solution)/shard_map/cond
  434.1 36.3 %collective-permute-start.25 = (bf16[4096,768]{1,0:T(8,128)(2,1)}, bf16[4096,768]{1,0:T(8,128)(2,1)}, u32[]{:S(2)}, u32[]{:S(2)}) collective-permute-start(bf16[4096,768]{1,0:T(8,128)(2,1)} %branch_2_fun.17.refs_1_.refs_0_), channel_id=1, source_target_pairs={{0,1},{1,0},{2,3},{3,2},{4,5},{5,4},{6,7},{7,6}} | collective-permute-start | bytes 18874376 | tf_op jit(solution)/shard_map/cond/branch_2_fun/ppermute | solution.py:313
  434.9 18.2 %copy-start.5 = (s32[8192]{0:T(1024)S(1)}, s32[8192]{0:T(1024)}, u32[]{:S(2)}) copy-start(s32[8192]{0:T(1024)} %copy-done.4) | copy-start | bytes 98308 | tf_op jit(solution)/shard_map/cond
  434.9 18.2 %copy-start.23 = (s32[8192]{0:T(1024)S(1)}, s32[8192]{0:T(1024)}, u32[]{:S(2)}) copy-start(s32[8192]{0:T(1024)} %copy-done.22) | copy-start | bytes 98308 | tf_op jit(solution)/shard_map/cond
  434.9 18.2 %copy-start.41 = (s32[8192]{0:T(1024)S(1)}, s32[8192]{0:T(1024)}, u32[]{:S(2)}) copy-start(s32[8192]{0:T(1024)} %copy-done.40) | copy-start | bytes 98308 | tf_op jit(solution)/shard_map/cond
  434.9 18.2 %copy-start.59 = (s32[8192]{0:T(1024)S(1)}, s32[8192]{0:T(1024)}, u32[]{:S(2)}) copy-start(s32[8192]{0:T(1024)} %copy-done.58) | copy-start | bytes 98308 | tf_op jit(solution)/shard_map/cond
  434.9 18.2 %copy-start.74 = (s32[8192]{0:T(1024)S(1)}, s32[8192]{0:T(1024)}, u32[]{:S(2)}) copy-start(s32[8192]{0:T(1024)} %get-tuple-element.1482) | copy-start | bytes 98308 | tf_op jit(solution)/shard_map/cond
  434.9 18.2 %copy-start.83 = (s32[8192]{0:T(1024)S(1)}, s32[8192]{0:T(1024)}, u32[]{:S(2)}) copy-start(s32[8192]{0:T(1024)} %get-tuple-element.942) | copy-start | bytes 98308 | tf_op jit(solution)/shard_map/cond
  434.9 18.2 %copy-start.92 = (s32[8192]{0:T(1024)S(1)}, s32[8192]{0:T(1024)}, u32[]{:S(2)}) copy-start(s32[8192]{0:T(1024)} %get-tuple-element.1005) | copy-start | bytes 98308 | tf_op jit(solution)/shard_map/cond
  452.4 86.3 %collective-permute-start.26 = (bf16[2560,768]{1,0:T(8,128)(2,1)}, bf16[2560,768]{1,0:T(8,128)(2,1)}, u32[]{:S(2)}, u32[]{:S(2)}) collective-permute-start(bf16[2560,768]{1,0:T(8,128)(2,1)} %branch_2_fun.18), channel_id=1, source_target_pairs={{0,2},{1,3},{2,0},{3,1},{4,6},{5,7},{6,4},{7,5}} | collective-permute-start | bytes 11796488 | tf_op jit(solution)/shard_map/cond/branch_2_fun/ppermute | solution.py:313
  487.7 135.3 %collective-permute-start.28 = (bf16[2560,768]{1,0:T(8,128)(2,1)}, bf16[2560,768]{1,0:T(8,128)(2,1)}, u32[]{:S(2)}, u32[]{:S(2)}) collective-permute-start(bf16[2560,768]{1,0:T(8,128)(2,1)} %branch_2_fun.20), channel_id=1, source_target_pairs={{0,2},{1,3},{2,0},{3,1},{4,6},{5,7},{6,4},{7,5}} | collective-permute-start | bytes 11796488 | tf_op jit(solution)/shard_map/cond/branch_2_fun/ppermute | solution.py:313
  538.7 85.6 %collective-permute-start.27 = (bf16[2560,768]{1,0:T(8,128)(2,1)}, bf16[2560,768]{1,0:T(8,128)(2,1)}, u32[]{:S(2)}, u32[]{:S(2)}) collective-permute-start(bf16[2560,768]{1,0:T(8,128)(2,1)} %collective-permute-done.26.refs_4_), channel_id=1, source_target_pairs={{0,1},{1,0},{2,3},{3,2},{4,5},{5,4},{6,7},{7,6}} | collective-permute-start | bytes 11796488 | tf_op jit(solution)/shard_map/cond/branch_2_fun/ppermute | solution.py:313
  622.9 81.9 %collective-permute-start.29 = (bf16[2560,768]{1,0:T(8,128)(2,1)}, bf16[2560,768]{1,0:T(8,128)(2,1)}, u32[]{:S(2)}, u32[]{:S(2)}) collective-permute-start(bf16[2560,768]{1,0:T(8,128)(2,1)} %collective-permute-done.28.refs_0_), channel_id=1, source_target_pairs={{0,1},{1,0},{2,3},{3,2},{4,5},{5,4},{6,7},{7,6}} | collective-permute-start | bytes 11796488 | tf_op jit(solution)/shard_map/cond/branch_2_fun/ppermute | solution.py:313
  (15 other events, 173.7 us)

commit v4 on v3

--- a/solution.py
+++ b/solution.py
@@ -10,8 +10,10 @@
 
 LANES = 128
 ROW = 6
-BLOCK = 512
-WINDOW = BLOCK // 2 + 16
+BLOCK = 256
+WIDE = 512
+WINDOW = WIDE // 2 + 16
+GROUP = 16
 FAR = 1 << 20
 VMEM = 61 * 2**20
 FF_CHUNK = 768
@@ -62,10 +64,6 @@
     return pl.CostEstimate(flops=int(flops), bytes_accessed=int(size), transcendentals=0)
 
 
-def blocks_of(rows):
-    return -(-rows // BLOCK)
-
-
 def phases(counts):
     first = [0]
     for c in counts:
@@ -74,93 +72,130 @@
 
 
 def split_rows(ref, rows, base):
+    size = ref.shape[0]
     for k in range(ref.shape[1] // LANES):
-        rows[pl.ds(base + k, BLOCK, stride=ROW), :] = ref[:, k * LANES:(k + 1) * LANES].astype(jnp.float32)
+        rows[pl.ds(base + k, size, stride=ROW), :] = ref[:, k * LANES:(k + 1) * LANES].astype(jnp.float32)
 
 
 def join_rows(rows, base, ref):
+    size = ref.shape[0]
     for k in range(ref.shape[1] // LANES):
-        ref[:, k * LANES:(k + 1) * LANES] = rows[pl.ds(base + k, BLOCK, stride=ROW), :].astype(ref.dtype)
+        ref[:, k * LANES:(k + 1) * LANES] = rows[pl.ds(base + k, size, stride=ROW), :].astype(ref.dtype)
 
 
 def line(r):
     return pl.ds(r * ROW, ROW)
 
 
-def compact_kernel(first, last, base_ref, pos_ref, *refs):
-    parts, out_ref, acc = refs[:-2], refs[-2], refs[-1]
-    i = pl.program_id(0)
-
-    @pl.when(i == 0)
-    def _():
-        acc[...] = jnp.zeros_like(acc)
-
-    base = pl.multiple_of(base_ref[i], 16)
-    spots = lax.broadcasted_iota(jnp.int32, (WINDOW, BLOCK), 0) + base
-    pick = jnp.where(spots == pos_ref[0], 1.0, 0.0).astype(jnp.bfloat16)
-    for lo, hi, ref in zip(first[:-1], first[1:], parts):
-        @pl.when((i >= lo) & (i < hi))
-        def _(ref=ref):
-            moved = jnp.dot(pick, ref[...], preferred_element_type=jnp.float32)
+def stream(parts, bodies, ring, sems):
+    depth, block = ring.shape[0], ring.shape[1]
+    first = phases([p.shape[0] // block for p in parts])
+    total = first[-1]
+
+    def copy(p, step):
+        slot = step % depth
+        return pltpu.make_async_copy(parts[p].at[pl.ds((step - first[p]) * block, block), :], ring.at[slot], sems.at[slot])
+
+    for s in range(min(depth - 1, total)):
+        copy(max(p for p in range(len(parts)) if first[p] <= s), s).start()
+    for p, body in enumerate(bodies):
+        def run(step, c, p=p, body=body):
+            copy(p, step).wait()
+            ahead = step + depth - 1
+            for q in range(p, len(parts)):
+                @pl.when((ahead >= first[q]) & (ahead < first[q + 1]))
+                def _(q=q):
+                    copy(q, ahead).start()
+            body(step - first[p], ring.at[step % depth])
+            return c
+
+        lax.fori_loop(first[p], first[p + 1], run, 0)
+
+
+def drain(acc, out_ref, stage, sems):
+    depth, block = stage.shape[0], stage.shape[1]
+    total = out_ref.shape[0] // block
+
+    def copy(j):
+        return pltpu.make_async_copy(stage.at[j % depth], out_ref.at[pl.ds(j * block, block), :], sems.at[j % depth])
+
+    def run(j, c):
+        @pl.when(j >= depth)
+        def _():
+            copy(j - depth).wait()
+
+        join_rows(acc, j * block * ROW, stage.at[j % depth])
+        copy(j).start()
+        return c
+
+    lax.fori_loop(0, total, run, 0)
+    for j in range(max(0, total - depth), total):
+        copy(j).wait()
+
+
+def ring_of(block, d, depth, dtype=jnp.bfloat16):
+    return [pltpu.VMEM((depth, block, d), dtype), pltpu.SemaphoreType.DMA((depth,))]
+
+
+def compact_kernel(base_ref, pos_ref, *refs):
+    parts, (out_ref, acc, ring, sems) = refs[:-4], refs[-4:]
+    acc[...] = jnp.zeros_like(acc)
+    first = phases([p.shape[0] // WIDE for p in parts])
+
+    def body_of(p):
+        def body(b, rows):
+            b = b + first[p]
+            base = pl.multiple_of(base_ref[b], 16)
+            spots = lax.broadcasted_iota(jnp.int32, (WINDOW, WIDE), 0) + base
+            pick = jnp.where(spots == pos_ref[b], 1.0, 0.0).astype(jnp.bfloat16)
+            moved = jnp.dot(pick, rows[...], preferred_element_type=jnp.float32)
             acc[pl.ds(base, WINDOW), :] = acc[pl.ds(base, WINDOW), :] + moved
 
-    @pl.when(i == last)
-    def _():
-        out_ref[...] = acc[0:out_ref.shape[0], :].astype(out_ref.dtype)
+        return body
+
+    stream(parts, [body_of(p) for p in range(len(parts))], ring, sems)
+    out_ref[...] = acc[0:out_ref.shape[0], :].astype(out_ref.dtype)
 
 
 def compact(parts, pos, rows):
     d = parts[0].shape[1]
-    counts = [p.shape[0] // BLOCK for p in parts]
-    first = phases(counts)
-    pos = pos.reshape(-1, BLOCK)
+    pos = pos.reshape(-1, WIDE)
     low = jnp.where(pos >= 0, pos, FAR).min(1)
     base = jnp.where(low < FAR, jnp.minimum(low, rows) // 16 * 16, 0)
-
-    def spec(k):
-        return pl.BlockSpec((BLOCK, d), lambda i, *_: (jnp.clip(i - first[k], 0, counts[k] - 1), 0))
-
+    hbm = pl.BlockSpec(memory_space=pl.ANY)
     return call(
-        functools.partial(compact_kernel, first, first[-1] - 1), base, pos[:, None, :], *parts,
+        compact_kernel, base, pos[:, None, :], *parts,
         grid_spec=pltpu.PrefetchScalarGridSpec(
             num_scalar_prefetch=1,
-            grid=(first[-1],),
-            in_specs=[pl.BlockSpec((1, 1, BLOCK), lambda i, *_: (i, 0, 0))] + [spec(k) for k in range(len(parts))],
+            grid=(1,),
+            in_specs=[pl.BlockSpec((pos.shape[0], 1, WIDE), lambda i, *_: (0, 0, 0))] + [hbm] * len(parts),
             out_specs=pl.BlockSpec((rows, d), lambda i, *_: (0, 0)),
-            scratch_shapes=[pltpu.VMEM((rows + WINDOW, d), jnp.float32)],
+            scratch_shapes=[pltpu.VMEM((rows + WINDOW, d), jnp.float32)] + ring_of(WIDE, d, 6),
         ),
         out_shape=jax.ShapeDtypeStruct((rows, d), parts[0].dtype),
         cost_estimate=cost(2e10, 2 * d * (sum(p.shape[0] for p in parts) + rows)),
     )
 
 
-def gather_kernel(first, stride, has_init, pos_ref, slot_ref, start_ref, *refs):
-    refs, out_ref, acc, rows = refs[:-3], refs[-3], refs[-2], refs[-1]
-    i = pl.program_id(0)
-    if has_init:
-        @pl.when(i < first[1])
-        def _():
-            split_rows(refs[0], acc, i * BLOCK * ROW)
-
-        refs, first = refs[1:], first[1:]
-    else:
-        @pl.when(i == 0)
-        def _():
-            acc[...] = jnp.zeros_like(acc)
-
-    for p, ref in enumerate(refs):
-        @pl.when((i >= first[p]) & (i < first[p + 1]))
-        def _(p=p, ref=ref):
-            split_rows(ref, rows, 0)
-            v = p * stride + i - first[p]
+def gather_kernel(stride, init_at, pos_ref, slot_ref, start_ref, *refs):
+    parts, (out_ref, acc, rows, ring, sems, stage, out_sems) = list(refs[:-7]), refs[-7:]
+    bodies = []
+    if init_at is not None:
+        parts[0] = parts[0].at[pl.ds(init_at, out_ref.shape[0]), :]
+        bodies.append(lambda b, src: split_rows(src, acc, b * BLOCK * ROW))
+
+    def body_of(p):
+        def body(b, src):
+            split_rows(src, rows, 0)
+            v = p * stride + b
             low = v * BLOCK
             start, end = start_ref[v], start_ref[v + 1]
-            full = (end - start) // 8
-
-            def eight(j, c):
-                at = start + j * 8
-                values = [rows[line(pos_ref[at + u] - low), :] for u in range(8)]
-                for u in range(8):
+            full = (end - start) // GROUP
+
+            def many(j, c):
+                at = start + j * GROUP
+                values = [rows[line(pos_ref[at + u] - low), :] for u in range(GROUP)]
+                for u in range(GROUP):
                     acc[line(slot_ref[at + u]), :] = values[u]
                 return c
 
@@ -168,42 +203,35 @@
                 acc[line(slot_ref[j]), :] = rows[line(pos_ref[j] - low), :]
                 return c
 
-            lax.fori_loop(0, full, eight, 0)
-            lax.fori_loop(start + full * 8, end, single, 0)
-
-    @pl.when(i >= first[len(refs)])
-    def _():
-        join_rows(acc, (i - first[len(refs)]) * BLOCK * ROW, out_ref)
+            lax.fori_loop(0, full, many, 0)
+            lax.fori_loop(start + full * GROUP, end, single, 0)
+
+        return body
+
+    bodies += [body_of(p) for p in range(len(parts) - len(bodies))]
+    stream(parts, bodies, ring, sems)
+    drain(acc, out_ref, stage, out_sems)
 
 
 def gather(init, parts, key, slots, stride):
     d = parts[0].shape[1]
-    counts = [blocks_of(p.shape[0]) for p in parts]
-    has_init = init is not None
-    ins = list(parts)
-    if has_init:
-        counts, ins = [slots // BLOCK] + counts, [init[0]] + ins
-    counts = counts + [slots // BLOCK]
-    first = phases(counts)
     key, slot = lax.sort((key, jnp.arange(slots, dtype=jnp.int32)), num_keys=1)
     edges = jnp.arange(len(parts) * stride + 1, dtype=jnp.int32) * BLOCK
     starts = (key[None, :] < edges[:, None]).sum(1).astype(jnp.int32)
-
-    def spec(k, off=0):
-        return pl.BlockSpec((BLOCK, d), lambda i, *_: (jnp.clip(i - first[k], 0, counts[k] - 1) + off, 0))
-
-    offs = [init[1] if has_init else 0] + [0] * len(parts)
+    ins = ([init[0]] if init is not None else []) + list(parts)
+    hbm = pl.BlockSpec(memory_space=pl.ANY)
     return call(
-        functools.partial(gather_kernel, first, stride, has_init), key, slot, starts, *ins,
+        functools.partial(gather_kernel, stride, None if init is None else init[1]), key, slot, starts, *ins,
         grid_spec=pltpu.PrefetchScalarGridSpec(
             num_scalar_prefetch=3,
-            grid=(first[-1],),
-            in_specs=[spec(k, offs[k]) for k in range(len(ins))],
-            out_specs=spec(len(counts) - 1),
-            scratch_shapes=[pltpu.VMEM((slots * ROW, LANES), jnp.float32), pltpu.VMEM((BLOCK * ROW, LANES), jnp.float32)],
+            grid=(1,),
+            in_specs=[hbm] * len(ins),
+            out_specs=hbm,
+            scratch_shapes=[pltpu.VMEM((slots * ROW, LANES), jnp.float32), pltpu.VMEM((BLOCK * ROW, LANES), jnp.float32)]
+            + ring_of(BLOCK, d, 8) + ring_of(BLOCK, d, 4),
         ),
         out_shape=jax.ShapeDtypeStruct((slots, d), parts[0].dtype),
-        cost_estimate=cost(4e10, 2 * d * (sum(p.shape[0] for p in ins) + slots)),
+        cost_estimate=cost(4e10, 2 * d * (sum(p.shape[0] for p in parts) + 2 * slots)),
     )
 
 
@@ -237,70 +265,82 @@
     )
 
 
-def combine_kernel(first, dest_ref, dup_ref, tok_ref, *refs):
-    parts, out_ref, acc, rows = refs[:-3], refs[-3], refs[-2], refs[-1]
-    i = pl.program_id(0)
-
-    @pl.when(i < first[1])
-    def _():
-        split_rows(tok_ref, acc, i * BLOCK * ROW)
-
-    for p, ref in enumerate(parts):
-        @pl.when((i >= first[p + 1]) & (i < first[p + 2]))
-        def _(ref=ref):
-            step = i - first[1]
-            start = step * BLOCK
-            split_rows(ref, rows, 0)
-
-            @pl.when(dup_ref[step] == 0)
-            def _():
-                def body(j, c):
-                    where = [line(dest_ref[start + j * 8 + u]) for u in range(8)]
-                    sums = [acc[where[u], :] + rows[line(j * 8 + u), :] for u in range(8)]
-                    for u in range(8):
-                        acc[where[u], :] = sums[u]
-                    return c
-
-                lax.fori_loop(0, BLOCK // 8, body, 0)
-
-            @pl.when(dup_ref[step] != 0)
-            def _():
-                def body(r, c):
-                    w = line(dest_ref[start + r])
-                    acc[w, :] = acc[w, :] + rows[line(r), :]
-                    return c
-
-                lax.fori_loop(0, BLOCK, body, 0)
-
-    @pl.when(i >= first[-2])
-    def _():
-        join_rows(acc, (i - first[-2]) * BLOCK * ROW, out_ref)
-
-
-def combine(init, parts, dests, dtype):
-    n, d = init.shape
-    counts = [n // BLOCK] + [blocks_of(p.shape[0]) for p in parts] + [n // BLOCK]
-    first = phases(counts)
-    dest = jnp.concatenate([jnp.pad(x[:p.shape[0]], (0, -p.shape[0] % BLOCK), constant_values=n) for p, x in zip(parts, dests)])
-    groups = dest.reshape(-1, 8)
-    same = jnp.zeros(groups.shape[:1], bool)
-    for u in range(1, 8):
-        same |= ((groups[:, u:] == groups[:, :-u]) & (groups[:, u:] < n)).any(1)
-    dup = same.reshape(-1, BLOCK // 8).any(1).astype(jnp.int32)
-
-    def spec(k):
-        return pl.BlockSpec((BLOCK, d), lambda i, *_: (jnp.clip(i - first[k], 0, counts[k] - 1), 0))
-
+def combine_kernel(flagged, init_rows, dest_ref, dup_ref, *refs):
+    parts, (out_ref, acc, rows, ring, sems, stage, out_sems, acc_sem) = list(refs[:-8]), refs[-8:]
+    bodies = []
+    n = acc.shape[0] // ROW - 1
+    held = acc.at[pl.ds(0, n * ROW), :]
+    if init_rows:
+        load = pltpu.make_async_copy(parts.pop(0), held, acc_sem)
+        load.start()
+    else:
+        bodies.append(lambda b, src: split_rows(src, acc, b * BLOCK * ROW))
+    skip = len(bodies)
+    first = phases([p.shape[0] // BLOCK for p in parts[skip:]])
+
+    def add(start, width):
+        def body(j, c):
+            at = j * width
+            where = [line(dest_ref[start + at + u]) for u in range(width)]
+            sums = [acc[where[u], :] + rows[line(at + u), :] for u in range(width)]
+            for u in range(width):
+                acc[where[u], :] = sums[u]
+            return c
+
+        lax.fori_loop(0, BLOCK // width, body, 0)
+
+    def body_of(p):
+        def body(b, src):
+            split_rows(src, rows, 0)
+            step = first[p] + b
+            if not flagged[p]:
+                add(step * BLOCK, GROUP)
+                return
+            for flag, width in ((0, GROUP), (1, 8), (2, 1)):
+                @pl.when(dup_ref[step] == flag)
+                def _(width=width):
+                    add(step * BLOCK, width)
+
+        return body
+
+    bodies += [body_of(p) for p in range(len(flagged))]
+    if init_rows:
+        load.wait()
+    stream(parts, bodies, ring, sems)
+    if init_rows:
+        drain(acc, out_ref, stage, out_sems)
+    else:
+        save = pltpu.make_async_copy(held, out_ref, acc_sem)
+        save.start()
+        save.wait()
+
+
+def combine(init, parts, dests, flagged, n):
+    d = parts[0].shape[1]
+    init_rows = init.dtype == jnp.float32
+    dest = jnp.concatenate([x[:p.shape[0]] for p, x in zip(parts, dests)])
+
+    def twice(width):
+        g = dest.reshape(-1, width)
+        same = jnp.zeros(g.shape[:1], bool)
+        for u in range(1, width):
+            same |= ((g[:, u:] == g[:, :-u]) & (g[:, u:] < n)).any(1)
+        return same.reshape(-1, BLOCK // width).any(1)
+
+    dup = jnp.where(twice(8), 2, jnp.where(twice(GROUP), 1, 0)).astype(jnp.int32)
+    hbm = pl.BlockSpec(memory_space=pl.ANY)
+    out = jax.ShapeDtypeStruct((n, d), parts[0].dtype) if init_rows else jax.ShapeDtypeStruct((n * ROW, LANES), jnp.float32)
     return call(
-        functools.partial(combine_kernel, first), dest, dup, init, *parts,
+        functools.partial(combine_kernel, flagged, init_rows), dest, dup, init, *parts,
         grid_spec=pltpu.PrefetchScalarGridSpec(
             num_scalar_prefetch=2,
-            grid=(first[-1],),
-            in_specs=[spec(k) for k in range(len(parts) + 1)],
-            out_specs=spec(len(parts) + 1),
-            scratch_shapes=[pltpu.VMEM(((n + 1) * ROW, LANES), jnp.float32), pltpu.VMEM((BLOCK * ROW, LANES), jnp.float32)],
+            grid=(1,),
+            in_specs=[hbm] * (len(parts) + 1),
+            out_specs=hbm,
+            scratch_shapes=[pltpu.VMEM(((n + 1) * ROW, LANES), jnp.float32), pltpu.VMEM((BLOCK * ROW, LANES), jnp.float32)]
+            + ring_of(BLOCK, d, 8) + ring_of(BLOCK, d, 4) + [pltpu.SemaphoreType.DMA],
         ),
-        out_shape=jax.ShapeDtypeStruct((n, d), dtype),
+        out_shape=out,
         cost_estimate=cost(1e11, 2 * d * dest.shape[0]),
     )
 
@@ -329,7 +369,7 @@
         me = lax.axis_index("ep")
         chip, core = me // 2, me % 2
         chip_n = 2 * n
-        levels = [(min(part, -(-(L * 15 // 16) // 128) * 128), min(part, -(-(L * 13 // 16) // 128) * 128), L) for L in range(2048, part, 256)]
+        levels = [(min(part, -(-(L * 15 // 16) // 256) * 256), min(part, -(-(L * 13 // 16) // 256) * 256), L) for L in range(2048, part, 256)]
         levels.append((part, part, part))
 
         def by_turn(x):
@@ -391,7 +431,7 @@
                     key = (late * 2 + jnp.where(rank % 2 == core, 0, 1)) * part + rank // 2
                     key = jnp.where(is_far, key, FAR)
                     tables = [t for k in range(h + 1) for t in (got[k], sib_got[k])]
-                    x.append(gather((x_near, h * (part // BLOCK)), tables, key, part, part // BLOCK))
+                    x.append(gather((x_near, h * part), tables, key, part, part // BLOCK))
                     p.append(ffn(x[h], w_in, w_out, gate[h], h, turns))
                 sib_p = [hop(y, swap_core) for y in p]
                 back = [compact([p[h], sib_p[h]], my_turn(back_far[h], back_rank[h]), rows[2]) for h in range(turns)]
@@ -407,8 +447,8 @@
                 own_to = [place(mine[h] - me * n) for h in range(turns)]
                 sib_to = [place(sib[h] - me * n) for h in range(turns)]
                 acc = combine(tok, [p[0], p[1], sib_p[0], sib_p[1], back_got[0], sib_back[0]],
-                              [own_to[0], own_to[1], sib_to[0], sib_to[1]] + come[0], jnp.float32)
-                return combine(acc, [back_got[1], sib_back[1]], come[1], tok.dtype)
+                              [own_to[0], own_to[1], sib_to[0], sib_to[1]] + come[0], (False,) * 4 + (True,) * 2, n)
+                return combine(acc, [back_got[1], sib_back[1]], come[1], (True,) * 2, n)
 
             return run
 

time: 778 us -> 693 us (0.89)
  Pallas kernels: 423 us -> 334 us
  other arithmetic: 43 us -> 51.5 us
    pallas_call x11, Pallas kernels: 423 us -> 334 us  [call(): pl.pallas_call(kernel, compiler_params=pltpu.CompilerParams(dimension_sem...]
    reduce_or x14 -> x44, other arithmetic: 6.14 us -> 14.5 us  [the longest x40 14.1 us: twice(): same |= ((g[:, u:] == g[:, :-u]) & (g[:, u:] < n)).any(1)]
  transfers between devices with their start and end apart: 13 -> 13, of which waited for: 5 -> 4; matrix products, arithmetic and copies ran while one was open for 15% -> 18% of each run, Pallas kernels for 47% -> 42%
where the time goes in v4:
time: 693 us; the launch traced here: 683 us
  Pallas kernels  334 us (48%)
  waiting for transfers between devices  171 us (25%)
  other arithmetic  51.5 us (7%)
  local copies, waits for them, and re-layouts  40.7 us (6%)
  matrix products  34.2 us (5%)
  loops' own time  26.9 us (4%)
  starting transfers between devices  17 us (2%)
  between operations  7.37 us (1%)
    pallas_call x11, Pallas kernels, call(): pl.pallas_call(kernel, compiler_params=pltpu.CompilerParams(dimension_sem...  334 us
    ppermute x10, waiting for transfers between devices, hop(): return lax.ppermute(x, 'ep', pairs)  158 us
    dot_general x28, matrix products, bdot(): jnp.einsum(spec, a.astype(jnp.bfloat16), b.astype(jnp.bfloat16), preferre...  34.2 us
    another operation x1, loops' own time, local_layer(): lax.switch(level, branches, tok_loc, sib_tok, give_pos, want, want_rank,...  26.9 us
    sort x3, other arithmetic, gather(): key, slot = lax.sort((key, jnp.arange(slots, dtype=jnp.int32)), num_keys=1)  18.3 us
    reduce_or x40, other arithmetic, twice(): same |= ((g[:, u:] == g[:, :-u]) & (g[:, u:] < n)).any(1)  14.1 us
  transfers between devices with their start and end apart: 13, of which 4 were waited for; matrix products, arithmetic and copies ran while one was open for 18% of the time, Pallas kernels for 42%

profile of v4, /device:TPU:5, one launch (start us, length us, event | category | flops | bytes accessed | tf_op | source)
XLA Modules:
  0.0 682.9 jit_solution(3625844667800412731)
XLA Ops:
  2.2 3.9 all-to-all-start
  7.0 12.9 %all-to-all-done = s32[4,2,4096]{2,1,0:T(2,128)} async-done(((s32[4,2,4096]{2,1,0:T(2,128)}), s32[4,2,4096]{2,1,0:T(2,128)}, u32[]{:S(2)}, u32[]{:S(2)}) %all-to-all-start) | async-done | bytes 131104 | tf_op jit(solution)/shard_map/all_to_all | solution.py:349
  25.0 4.1 convert_reduce_fusion.31
  29.1 4.1 convert_reduce_fusion.27
  34.1 4.1 convert_reduce_fusion.29
  38.3 4.1 fusion.2468
  46.5 3.5 all-to-all-start.1
  58.2 623.6 %conditional.1 = (bf16[8192,768]{1,0:T(8,128)(2,1)}) conditional(s32[]{:T(128)} %clamp.173, (s32[]{:T(128)}, s32[64,128]{1,0:T(8,128)S(1)}, s32[8192]{0:T(1024)S(1)}, s32[2,2,4096]{2,1,0:T(2,128)S(1)}, s32[]{:T(128)}, /*index=5*/s32[]{:T(128)}, s32[2,4096]{1,0:T(2,128)S(1)}, s32[]{:T(128)}, ...), branch_computations={%region_19.76_spmd, %region_76.133_spmd, %region_133.190_spmd, %re... | conditional | flops 478415093760 | bytes 839021312 | solution.py:457
  63.2 17.8 %branch_1_fun.12 = bf16[2304,768]{1,0:T(8,128)(2,1)} custom-call(s32[32]{0:T(128)} %get-tuple-element.17753.base_ref, s32[32,1,512]{2,1,0:T(1,128)} %reshape_reshape.77.pos_ref, bf16[8192,768]{1,0:T(8,128)(2,1)} %get-tuple-element.527.refs_0_, bf16[8192,768]{1,0:T(8,128)(2,1)} %get-tuple-element.535.refs_1_), custom_call_target="tpu_custom_call" | custom-call | flops 20000000000 | bytes 28704768 | tf_op jit(solution)/shard_map/cond/branch_1_fun/pallas_call | solution.py:60
  82.9 18.1 %branch_1_fun.15 = bf16[2048,768]{1,0:T(8,128)(2,1)} custom-call(s32[32]{0:T(128)} %get-tuple-element.17752.base_ref, s32[32,1,512]{2,1,0:T(1,128)} %reshape_reshape.79.pos_ref, bf16[8192,768]{1,0:T(8,128)(2,1)} %get-tuple-element.527.refs_0_, bf16[8192,768]{1,0:T(8,128)(2,1)} %get-tuple-element.535.refs_1_), custom_call_target="tpu_custom_call" | custom-call | flops 20000000000 | bytes 28311552 | tf_op jit(solution)/shard_map/cond/branch_1_fun/pallas_call | solution.py:60
  103.9 2.4 fusion.318
  106.3 3.4 sub.1495
  109.8 2.4 fusion.333
  112.2 2.4 fusion.330
  114.6 3.5 sub.1481
  119.3 4.5 and_select_fusion.8
  133.7 9.4 %rev.43 = s32[2,4096]{1,0:T(2,128)} reverse(s32[2,4096]{1,0:T(2,128)S(1)} %reshape.5121), dimensions={0} | reverse | bytes 65536 | tf_op jit(solution)/shard_map/cond/branch_1_fun/rev | solution.py:410
  146.2 5.8 sort.381
  152.0 6.8 sort.382
  161.9 5.8 sort.383
  171.4 20.3 %branch_1_fun.11.refs_0_ = bf16[8192,768]{1,0:T(8,128)(2,1)} custom-call(s32[8192]{0:T(1024)} %copy-done.127, s32[8192]{0:T(1024)} %get-tuple-element.534.slot_ref, s32[65]{0:T(128)} %convert_reduce_fusion.3.start_ref, bf16[8192,768]{1,0:T(8,128)(2,1)} %get-tuple-element.527.refs_0_, bf16[8192,768]{1,0:T(8,128)(2,1)} %get-tuple-element.535.refs_1_), custom_call_target="tpu_custom_call" | custom-call | flops 40000000000 | bytes 50331648 | tf_op jit(solution)/shard_map/cond/branch_1_fun/pallas_call | solution.py:60
  191.7 34.8 %collective-permute-done.12.refs_3_ = bf16[2048,768]{1,0:T(8,128)(2,1)} collective-permute-done((bf16[2048,768]{1,0:T(8,128)(2,1)}, bf16[2048,768]{1,0:T(8,128)(2,1)}, u32[]{:S(2)}, u32[]{:S(2)}) %collective-permute-start.12) | collective-permute-done | bytes 3145760 | tf_op jit(solution)/shard_map/cond/branch_1_fun/ppermute | solution.py:353
  227.7 20.0 %branch_1_fun.13.x_ref = bf16[4096,768]{1,0:T(8,128)(2,1)} custom-call(s32[4096]{0:T(1024)} %copy-done.143, s32[4096]{0:T(1024)} %get-tuple-element.532.slot_ref, s32[33]{0:T(128)} %convert_reduce_fusion.5.start_ref, bf16[8192,768]{1,0:T(8,128)(2,1)} %branch_1_fun.11.refs_0_, bf16[2304,768]{1,0:T(8,128)(2,1)} %collective-permute-done.10.refs_1_, ...), custom_call_target="tpu_custom_call" | custom-call | flops 40000000000 | bytes 19660800 | tf_op jit(solution)/shard_map/cond/branch_1_fun/pallas_call | solution.py:60
  247.8 60.5 %branch_1_fun.14.refs_0_.refs_1_ = bf16[4096,768]{1,0:T(8,128)(2,1)} custom-call(bf16[4096,768]{1,0:T(8,128)(2,1)} %branch_1_fun.13.x_ref, bf16[32,768,3072]{2,1,0:T(8,128)(2,1)} %get-tuple-element.1025.w_in_ref, bf16[32,3072,768]{2,1,0:T(8,128)(2,1)} %get-tuple-element.1034.w_out_ref, f32[16,256,1]{2,1,0:T(8,128)} %copy.1911.gate_ref), custom_call_target="tpu_custom_call" | custom-call | flops 38654705664 | bytes 150994944 | tf_op jit(solution)/shard_map/cond/branch_1_fun/pallas_call | solution.py:60
  308.3 22.9 %branch_1_fun.16.x_ref = bf16[4096,768]{1,0:T(8,128)(2,1)} custom-call(s32[4096]{0:T(1024)} %copy-done.144, s32[4096]{0:T(1024)} %get-tuple-element.541.slot_ref, s32[65]{0:T(128)} %convert_reduce_fusion.4.start_ref, bf16[8192,768]{1,0:T(8,128)(2,1)} %branch_1_fun.11.refs_0_, bf16[2304,768]{1,0:T(8,128)(2,1)} %collective-permute-done.10.refs_1_, ...), custom_call_target="tpu_custom_call" | custom-call | flops 40000000000 | bytes 25952256 | tf_op jit(solution)/shard_map/cond/branch_1_fun/pallas_call | solution.py:60
  331.3 61.0 %branch_1_fun.17.refs_2_.refs_0_ = bf16[4096,768]{1,0:T(8,128)(2,1)} custom-call(bf16[4096,768]{1,0:T(8,128)(2,1)} %branch_1_fun.16.x_ref, bf16[32,768,3072]{2,1,0:T(8,128)(2,1)} %get-tuple-element.1025.w_in_ref, bf16[32,3072,768]{2,1,0:T(8,128)(2,1)} %get-tuple-element.1034.w_out_ref, f32[16,256,1]{2,1,0:T(8,128)} %copy.1912.gate_ref), custom_call_target="tpu_custom_call" | custom-call | flops 38654705664 | bytes 150994944 | tf_op jit(solution)/shard_map/cond/branch_1_fun/pallas_call | solution.py:60
  401.8 11.3 %branch_1_fun.18 = bf16[2304,768]{1,0:T(8,128)(2,1)} custom-call(s32[16]{0:T(128)} %compare_select_fusion.31.base_ref, s32[16,1,512]{2,1,0:T(1,128)} %reshape.5119.pos_ref, bf16[4096,768]{1,0:T(8,128)(2,1)} %branch_1_fun.14.refs_0_.refs_1_, bf16[4096,768]{1,0:T(8,128)(2,1)} %collective-permute-done.14.refs_1_.refs_3_), custom_call_target="tpu_custom_call" | custom-call | flops 20000000000 | bytes 16121856 | tf_op jit(solution)/shard_map/cond/branch_1_fun/pallas_call | solution.py:60
  417.3 11.4 %branch_1_fun.20 = bf16[2304,768]{1,0:T(8,128)(2,1)} custom-call(s32[16]{0:T(128)} %compare_select_fusion.30.base_ref, s32[16,1,512]{2,1,0:T(1,128)} %reshape.5123.pos_ref, bf16[4096,768]{1,0:T(8,128)(2,1)} %branch_1_fun.17.refs_2_.refs_0_, bf16[4096,768]{1,0:T(8,128)(2,1)} %collective-permute-done.15.refs_4_.refs_1_), custom_call_target="tpu_custom_call" | custom-call | flops 20000000000 | bytes 16121856 | tf_op jit(solution)/shard_map/cond/branch_1_fun/pallas_call | solution.py:60
  430.1 60.9 %collective-permute-done.16.refs_5_ = bf16[2304,768]{1,0:T(8,128)(2,1)} collective-permute-done((bf16[2304,768]{1,0:T(8,128)(2,1)}, bf16[2304,768]{1,0:T(8,128)(2,1)}, u32[]{:S(2)}, u32[]{:S(2)}) %collective-permute-start.16) | collective-permute-done | bytes 3538976 | tf_op jit(solution)/shard_map/cond/branch_1_fun/ppermute | solution.py:353
  504.2 62.7 %collective-permute-done.18.refs_1_ = bf16[2304,768]{1,0:T(8,128)(2,1)} collective-permute-done((bf16[2304,768]{1,0:T(8,128)(2,1)}, bf16[2304,768]{1,0:T(8,128)(2,1)}, u32[]{:S(2)}, u32[]{:S(2)}) %collective-permute-start.18) | collective-permute-done | bytes 3538976 | tf_op jit(solution)/shard_map/cond/branch_1_fun/ppermute | solution.py:353
  568.2 63.3 %branch_1_fun.19.refs_0_ = f32[49152,128]{1,0:T(8,128)} custom-call(s32[20992]{0:T(1024)} %copy-done.54, s32[82]{0:T(128)} %select_select_fusion.2.dup_ref, bf16[8192,768]{1,0:T(8,128)(2,1)} %get-tuple-element.527.refs_0_, bf16[4096,768]{1,0:T(8,128)(2,1)} %branch_1_fun.14.refs_0_.refs_1_, bf16[4096,768]{1,0:T(8,128)(2,1)} %branch_1_fun.17.refs_2_.refs_0_, ...), custom_call_target="tpu_custom_call" | custom-call | flops 99999997952 | bytes 32243712 | tf_op jit(solution)/shard_map/cond/branch_1_fun/pallas_call | solution.py:60
  631.5 27.3 %branch_1_fun.21 = bf16[8192,768]{1,0:T(8,128)(2,1)} custom-call(s32[4608]{0:T(1024)} %pad_add_fusion.3.dest_ref, s32[18]{0:T(128)} %select_select_fusion.3.dup_ref, f32[49152,128]{1,0:T(8,128)} %branch_1_fun.19.refs_0_, bf16[2304,768]{1,0:T(8,128)(2,1)} %collective-permute-done.18.refs_1_, bf16[2304,768]{1,0:T(8,128)(2,1)} %collective-permute-done.19.refs_2_), custom_call_target="tpu_custom_call" | custom-call | flops 99999997952 | bytes 7077888 | tf_op jit(solution)/shard_map/cond/branch_1_fun/pallas_call | solution.py:60
  (245 shorter events, 73.2 us)
Async XLA Ops:
  0.0 58.1 %collective-permute-start.90 = (bf16[8192,768]{1,0:T(8,128)(2,1)}, bf16[8192,768]{1,0:T(8,128)(2,1)}, u32[]{:S(2)}, u32[]{:S(2)}) collective-permute-start(bf16[8192,768]{1,0:T(8,128)(2,1)} %param.15), channel_id=1, source_target_pairs={{0,1},{1,0},{2,3},{3,2},{4,5},{5,4},{6,7},{7,6}} | collective-permute-start | bytes 37748744 | tf_op jit(solution)/shard_map/ppermute | solution.py:378
  2.2 17.7 %all-to-all-start = ((s32[4,2,4096]{2,1,0:T(2,128)}), s32[4,2,4096]{2,1,0:T(2,128)}, u32[]{:S(2)}, u32[]{:S(2)}) async-start(s32[4,2,4096]{2,1,0:T(2,128)} %broadcast_in_dim.1138), calls=%async_computation | async-start | bytes 262144 | tf_op jit(solution)/shard_map/all_to_all | solution.py:349
  38.3 6.2 copy-start.156
  46.5 10.3 %all-to-all-start.1 = ((s32[8,1,128]{2,1,0:T(1,128)}), s32[8,1,128]{2,1,0:T(1,128)S(1)}, u32[]{:S(2)}, u32[]{:S(2)}) async-start(s32[8,1,128]{2,1,0:T(1,128)} %broadcast_in_dim_broadcast_in_dim_broadcast_in_dim.3), calls=%async_computation.1 | async-start | bytes 8192 | tf_op jit(solution)/shard_map/all_to_all | solution.py:349
  81.0 89.4 %collective-permute-start.10 = (bf16[2304,768]{1,0:T(8,128)(2,1)}, bf16[2304,768]{1,0:T(8,128)(2,1)}, u32[]{:S(2)}, u32[]{:S(2)}) collective-permute-start(bf16[2304,768]{1,0:T(8,128)(2,1)} %branch_1_fun.12), channel_id=1, source_target_pairs={{0,2},{1,3},{2,0},{3,1},{4,6},{5,7},{6,4},{7,5}} | collective-permute-start | bytes 10616840 | tf_op jit(solution)/shard_map/cond/branch_1_fun/ppermute | solution.py:353
  101.0 125.4 %collective-permute-start.12 = (bf16[2048,768]{1,0:T(8,128)(2,1)}, bf16[2048,768]{1,0:T(8,128)(2,1)}, u32[]{:S(2)}, u32[]{:S(2)}) collective-permute-start(bf16[2048,768]{1,0:T(8,128)(2,1)} %branch_1_fun.15), channel_id=1, source_target_pairs={{0,2},{1,3},{2,0},{3,1},{4,6},{5,7},{6,4},{7,5}} | collective-permute-start | bytes 9437192 | tf_op jit(solution)/shard_map/cond/branch_1_fun/ppermute | solution.py:353
  125.2 8.4 %copy-start.77 = (s32[2304]{0:T(1024)}, s32[2304]{0:T(1024)S(1)}, u32[]{:S(2)}) copy-start(s32[2304]{0:T(1024)S(1)} %get-tuple-element.17626) | copy-start | bytes 27652 | tf_op jit(solution)/shard_map/cond
  125.2 8.4 %copy-start.79 = (s32[2304]{0:T(1024)}, s32[2304]{0:T(1024)S(1)}, u32[]{:S(2)}) copy-start(s32[2304]{0:T(1024)S(1)} %get-tuple-element.17627) | copy-start | bytes 27652 | tf_op jit(solution)/shard_map/cond
  133.7 9.5 %copy-start.65 = (s32[2,4096]{1,0:T(2,128)}, s32[2,4096]{1,0:T(2,128)S(1)}, u32[]{:S(2)}) copy-start(s32[2,4096]{1,0:T(2,128)S(1)} %reshape.5121) | copy-start | bytes 98308 | tf_op jit(solution)/shard_map/cond
  152.0 15.7 %copy-start.143 = (s32[4096]{0:T(1024)}, s32[4096]{0:T(1024)S(1)}, u32[]{:S(2)}) copy-start(s32[4096]{0:T(1024)S(1)} %get-tuple-element.531.pos_ref) | copy-start | bytes 49156 | tf_op jit(solution)/shard_map/cond
  158.8 10.6 %copy-start.127 = (s32[8192]{0:T(1024)}, s32[8192]{0:T(1024)S(1)}, u32[]{:S(2)}) copy-start(s32[8192]{0:T(1024)S(1)} %get-tuple-element.533.pos_ref) | copy-start | bytes 98308 | tf_op jit(solution)/shard_map/cond
  161.9 29.8 %copy-start.52 = (s32[20992]{0:T(1024)}, s32[20992]{0:T(1024)S(1)}, u32[]{:S(2)}) copy-start(s32[20992]{0:T(1024)S(1)} %get-tuple-element.17743) | copy-start | bytes 251908 | tf_op jit(solution)/shard_map/cond
  167.7 24.0 %copy-start.144 = (s32[4096]{0:T(1024)}, s32[4096]{0:T(1024)S(1)}, u32[]{:S(2)}) copy-start(s32[4096]{0:T(1024)S(1)} %get-tuple-element.540.pos_ref) | copy-start | bytes 49156 | tf_op jit(solution)/shard_map/cond
  170.4 57.3 %collective-permute-start.11 = (bf16[2304,768]{1,0:T(8,128)(2,1)}, bf16[2304,768]{1,0:T(8,128)(2,1)}, u32[]{:S(2)}, u32[]{:S(2)}) collective-permute-start(bf16[2304,768]{1,0:T(8,128)(2,1)} %collective-permute-done.10.refs_1_), channel_id=1, source_target_pairs={{0,1},{1,0},{2,3},{3,2},{4,5},{5,4},{6,7},{7,6}} | collective-permute-start | bytes 10616840 | tf_op jit(solution)/shard_map/cond/branch_1_fun/ppermute | solution.py:353
  226.5 81.9 %collective-permute-start.13 = (bf16[2048,768]{1,0:T(8,128)(2,1)}, bf16[2048,768]{1,0:T(8,128)(2,1)}, u32[]{:S(2)}, u32[]{:S(2)}) collective-permute-start(bf16[2048,768]{1,0:T(8,128)(2,1)} %collective-permute-done.12.refs_3_), channel_id=1, source_target_pairs={{0,1},{1,0},{2,3},{3,2},{4,5},{5,4},{6,7},{7,6}} | collective-permute-start | bytes 9437192 | tf_op jit(solution)/shard_map/cond/branch_1_fun/ppermute | solution.py:353
  308.3 93.5 %collective-permute-start.14 = (bf16[4096,768]{1,0:T(8,128)(2,1)}, bf16[4096,768]{1,0:T(8,128)(2,1)}, u32[]{:S(2)}, u32[]{:S(2)}) collective-permute-start(bf16[4096,768]{1,0:T(8,128)(2,1)} %branch_1_fun.14.refs_0_.refs_1_), channel_id=1, source_target_pairs={{0,1},{1,0},{2,3},{3,2},{4,5},{5,4},{6,7},{7,6}} | collective-permute-start | bytes 18874376 | tf_op jit(solution)/shard_map/cond/branch_1_fun/ppermute | solution.py:353
  331.2 61.2 %copy-start.66 = (s32[2,4096]{1,0:T(2,128)S(1)}, s32[2,4096]{1,0:T(2,128)}, u32[]{:S(2)}) copy-start(s32[2,4096]{1,0:T(2,128)} %copy-done.65) | copy-start | bytes 98308 | tf_op jit(solution)/shard_map/cond
  331.2 61.2 %copy-start.88 = (s32[2,4096]{1,0:T(2,128)S(1)}, s32[2,4096]{1,0:T(2,128)}, u32[]{:S(2)}) copy-start(s32[2,4096]{1,0:T(2,128)} %rev.43) | copy-start | bytes 98308 | tf_op jit(solution)/shard_map/cond
  331.2 61.9 %copy-start.35 = (s32[288,8]{1,0:T(8,128)S(1)}, s32[288,8]{1,0:T(8,128)}, u32[]{:S(2)}) copy-start(s32[288,8]{1,0:T(8,128)} %concatenate.87) | copy-start | bytes 27652 | tf_op jit(solution)/shard_map/cond
  331.3 61.9 %copy-start.36 = (s32[288,8]{1,0:T(8,128)S(1)}, s32[288,8]{1,0:T(8,128)}, u32[]{:S(2)}) copy-start(s32[288,8]{1,0:T(8,128)} %concatenate.96) | copy-start | bytes 27652 | tf_op jit(solution)/shard_map/cond
  331.3 62.0 %copy-start.71 = (s32[144,16]{1,0:T(8,128)S(1)}, s32[144,16]{1,0:T(8,128)}, u32[]{:S(2)}) copy-start(s32[144,16]{1,0:T(8,128)} %concatenate.98) | copy-start | bytes 27652 | tf_op jit(solution)/shard_map/cond
  331.3 62.1 %copy-start.72 = (s32[144,16]{1,0:T(8,128)S(1)}, s32[144,16]{1,0:T(8,128)}, u32[]{:S(2)}) copy-start(s32[144,16]{1,0:T(8,128)} %concatenate.99) | copy-start | bytes 27652 | tf_op jit(solution)/shard_map/cond
  331.3 62.2 %copy-start.17 = (s32[4096,2]{1,0:T(8,128)S(1)}, s32[4096,2]{1,0:T(8,128)}, u32[]{:S(2)}) copy-start(s32[4096,2]{1,0:T(8,128)} %get-tuple-element.17750) | copy-start | bytes 98308 | tf_op jit(solution)/shard_map/cond
  392.3 3.3 copy-start.53
  392.3 24.9 %collective-permute-start.15 = (bf16[4096,768]{1,0:T(8,128)(2,1)}, bf16[4096,768]{1,0:T(8,128)(2,1)}, u32[]{:S(2)}, u32[]{:S(2)}) collective-permute-start(bf16[4096,768]{1,0:T(8,128)(2,1)} %branch_1_fun.17.refs_2_.refs_0_), channel_id=1, source_target_pairs={{0,1},{1,0},{2,3},{3,2},{4,5},{5,4},{6,7},{7,6}} | collective-permute-start | bytes 18874376 | tf_op jit(solution)/shard_map/cond/branch_1_fun/ppermute | solution.py:353
  393.5 4.9 copy-start.89
  395.7 97.7 %copy-start.54 = (s32[20992]{0:T(1024)}, s32[20992]{0:T(1024)S(1)}, u32[]{:S(2)}) copy-start(s32[20992]{0:T(1024)S(1)} %constant_dynamic-update-slice_fusion.2.dest_ref) | copy-start | bytes 251908 | tf_op jit(solution)/shard_map/cond
  413.1 78.0 %collective-permute-start.16 = (bf16[2304,768]{1,0:T(8,128)(2,1)}, bf16[2304,768]{1,0:T(8,128)(2,1)}, u32[]{:S(2)}, u32[]{:S(2)}) collective-permute-start(bf16[2304,768]{1,0:T(8,128)(2,1)} %branch_1_fun.18), channel_id=1, source_target_pairs={{0,2},{1,3},{2,0},{3,1},{4,6},{5,7},{6,4},{7,5}} | collective-permute-start | bytes 10616840 | tf_op jit(solution)/shard_map/cond/branch_1_fun/ppermute | solution.py:353
  428.7 138.2 %collective-permute-start.18 = (bf16[2304,768]{1,0:T(8,128)(2,1)}, bf16[2304,768]{1,0:T(8,128)(2,1)}, u32[]{:S(2)}, u32[]{:S(2)}) collective-permute-start(bf16[2304,768]{1,0:T(8,128)(2,1)} %branch_1_fun.20), channel_id=1, source_target_pairs={{0,2},{1,3},{2,0},{3,1},{4,6},{5,7},{6,4},{7,5}} | collective-permute-start | bytes 10616840 | tf_op jit(solution)/shard_map/cond/branch_1_fun/ppermute | solution.py:353
  491.0 77.2 %collective-permute-start.17 = (bf16[2304,768]{1,0:T(8,128)(2,1)}, bf16[2304,768]{1,0:T(8,128)(2,1)}, u32[]{:S(2)}, u32[]{:S(2)}) collective-permute-start(bf16[2304,768]{1,0:T(8,128)(2,1)} %collective-permute-done.16.refs_5_), channel_id=1, source_target_pairs={{0,1},{1,0},{2,3},{3,2},{4,5},{5,4},{6,7},{7,6}} | collective-permute-start | bytes 10616840 | tf_op jit(solution)/shard_map/cond/branch_1_fun/ppermute | solution.py:353
  500.2 1.7 copy-start.80
  566.9 64.7 %collective-permute-start.19 = (bf16[2304,768]{1,0:T(8,128)(2,1)}, bf16[2304,768]{1,0:T(8,128)(2,1)}, u32[]{:S(2)}, u32[]{:S(2)}) collective-permute-start(bf16[2304,768]{1,0:T(8,128)(2,1)} %collective-permute-done.18.refs_1_), channel_id=1, source_target_pairs={{0,1},{1,0},{2,3},{3,2},{4,5},{5,4},{6,7},{7,6}} | collective-permute-start | bytes 10616840 | tf_op jit(solution)/shard_map/cond/branch_1_fun/ppermute | solution.py:353
  (1 other events, 1.7 us)
